TPU v7x, 8 devices: a whole 2x2x1 slice. The times are simulated.
8 devices in a mesh: dp: 2 (over z, y), cp: 4 (over x, core).
Axes of the slice: x: 2, y: 2, z: 1, core: 2. Of those that a mesh axis runs over, the one named last changes fastest.
Arguments:
- x_new: bfloat16 [1024, 3584], P(('dp', 'cp')), parts along dimension 0
- k_cache: bfloat16 [32768, 4, 128], P(('dp', 'cp')), parts along dimension 0
- v_cache: bfloat16 [32768, 4, 128], P(('dp', 'cp')), parts along dimension 0
- valid_len: int32 [8], P(('dp', 'cp')), parts along dimension 0
- w_q: bfloat16 [3584, 3584], replicated
- w_k: bfloat16 [3584, 512], replicated
- w_v: bfloat16 [3584, 512], replicated
- w_o: bfloat16 [3584, 3584], replicated
Outputs:
- output 1: bfloat16 [1024, 3584], P(('dp', 'cp')), parts along dimension 0
- output 2: bfloat16 [1024, 4, 128], P(('dp', 'cp')), parts along dimension 0
- output 3: bfloat16 [1024, 4, 128], P(('dp', 'cp')), parts along dimension 0
There are 2 independent parts. A program takes and returns all parts, laid end to end along the dimension named above; an argument that names none is the same for every part.
All inputs are finite; a program needn't handle non-finite values.
Results may differ from a plain program's by a relative error of at most 0.0107699.
Values are sent between devices in bfloat16 or wider.
A program may use at most 1 GiB of HBM per device.

v0:
```python
import jax
import jax.numpy as jnp
from jax import lax
from jax.sharding import PartitionSpec as P, NamedSharding

ROPE_BASE = 500000.0
NEG_BIG = -1e30


def rope_tables(positions, head_dim):
    half_dim = head_dim // 2
    inv_freq = jnp.power(ROPE_BASE, -jnp.arange(half_dim, dtype=jnp.float32) * (2.0 / head_dim))
    angles = positions.astype(jnp.float32)[:, None] * inv_freq[None, :]
    return jnp.cos(angles)[:, None, :], jnp.sin(angles)[:, None, :]


def rope_apply(values, cos_a, sin_a):
    half_dim = values.shape[-1] // 2
    first_half = values[..., :half_dim]
    second_half = values[..., half_dim:]
    return jnp.concatenate([first_half * cos_a - second_half * sin_a, second_half * cos_a + first_half * sin_a], axis=-1)


def segment_positions(dev_idx, tok_dev, cp_size):
    piece_len = tok_dev // 2
    within = jnp.arange(tok_dev)
    piece_ids = jnp.where(within < piece_len, dev_idx, 2 * cp_size - 1 - dev_idx)
    return piece_ids * piece_len + within % piece_len


def block_attend(q_blk, q_pos, k_ctx, v_ctx, ctx_len, k_seg, v_seg, key_pos):
    score_scale = q_blk.shape[-1] ** -0.5
    ctx_score = jnp.einsum('nkgd,skd->nkgs', q_blk, k_ctx, preferred_element_type=jnp.float32) * score_scale
    seg_score = jnp.einsum('nkgd,tkd->nkgt', q_blk, k_seg, preferred_element_type=jnp.float32) * score_scale
    ctx_ok = (jnp.arange(k_ctx.shape[0]) < ctx_len[0])[None, None, None, :]
    seg_ok = (key_pos[None, :] <= q_pos[:, None])[:, None, None, :]
    ctx_score = jnp.where(ctx_ok, ctx_score, NEG_BIG)
    seg_score = jnp.where(seg_ok, seg_score, NEG_BIG)
    blk_max = jnp.maximum(ctx_score.max(axis=-1), seg_score.max(axis=-1))
    ctx_wt = jnp.where(ctx_ok, jnp.exp(ctx_score - blk_max[..., None]), 0.0)
    seg_wt = jnp.where(seg_ok, jnp.exp(seg_score - blk_max[..., None]), 0.0)
    blk_sum = ctx_wt.sum(axis=-1) + seg_wt.sum(axis=-1)
    blk_out = jnp.einsum('nkgs,skd->nkgd', ctx_wt.astype(jnp.bfloat16), v_ctx, preferred_element_type=jnp.float32) + jnp.einsum('nkgt,tkd->nkgd', seg_wt.astype(jnp.bfloat16), v_seg, preferred_element_type=jnp.float32)
    return blk_max, blk_sum, blk_out


def solution(mesh):
    cp_size = mesh.shape['cp']
    shift_perm = [(source, (source + 1) % cp_size) for source in range(cp_size)]
    row_spec = P(('dp', 'cp'), None)
    cache_spec = P(('dp', 'cp'), None, None)
    len_spec = P(('dp', 'cp'))
    full_spec = P()

    def device_fn(x_new, k_cache, v_cache, valid_len, w_q, w_k, w_v, w_o):
        tok_dev = x_new.shape[0]
        cache_dev, kv_heads, head_dim = k_cache.shape
        heads = w_q.shape[1] // head_dim
        group = heads // kv_heads
        my_idx = lax.axis_index('cp')
        q_pos = segment_positions(my_idx, tok_dev, cp_size)
        cos_a, sin_a = rope_tables(cache_dev * cp_size + q_pos, head_dim)
        q_proj = jnp.dot(x_new, w_q, preferred_element_type=jnp.float32).reshape(tok_dev, heads, head_dim)
        q_loc = rope_apply(q_proj, cos_a, sin_a).astype(jnp.bfloat16).reshape(tok_dev, kv_heads, group, head_dim)
        k_proj = jnp.dot(x_new, w_k, preferred_element_type=jnp.float32).reshape(tok_dev, kv_heads, head_dim)
        k_new = rope_apply(k_proj, cos_a, sin_a).astype(jnp.bfloat16)
        v_new = jnp.dot(x_new, w_v, preferred_element_type=jnp.float32).astype(jnp.bfloat16).reshape(tok_dev, kv_heads, head_dim)
        run_max, run_sum, run_out = block_attend(q_loc, q_pos, k_cache, v_cache, valid_len, k_new, v_new, q_pos)

        def visit_step(step_idx, carry):
            k_ctx, v_ctx, ctx_len, k_seg, v_seg, old_max, old_sum, old_out = carry
            k_ctx = lax.ppermute(k_ctx, 'cp', shift_perm)
            v_ctx = lax.ppermute(v_ctx, 'cp', shift_perm)
            ctx_len = lax.ppermute(ctx_len, 'cp', shift_perm)
            k_seg = lax.ppermute(k_seg, 'cp', shift_perm)
            v_seg = lax.ppermute(v_seg, 'cp', shift_perm)
            source = (my_idx - step_idx) % cp_size
            key_pos = segment_positions(source, tok_dev, cp_size)
            blk_max, blk_sum, blk_out = block_attend(q_loc, q_pos, k_ctx, v_ctx, ctx_len, k_seg, v_seg, key_pos)
            new_max = jnp.maximum(old_max, blk_max)
            old_wt = jnp.exp(old_max - new_max)
            new_wt = jnp.exp(blk_max - new_max)
            new_sum = old_sum * old_wt + blk_sum * new_wt
            new_out = old_out * old_wt[..., None] + blk_out * new_wt[..., None]
            return (k_ctx, v_ctx, ctx_len, k_seg, v_seg, new_max, new_sum, new_out)

        final = lax.fori_loop(1, cp_size, visit_step, (k_cache, v_cache, valid_len, k_new, v_new, run_max, run_sum, run_out))
        attention = (final[7] / final[6][..., None]).astype(jnp.bfloat16).reshape(tok_dev, heads * head_dim)
        y_out = jnp.dot(attention, w_o, preferred_element_type=jnp.float32).astype(jnp.bfloat16)
        return y_out, k_new, v_new

    return jax.shard_map(device_fn, mesh=mesh, in_specs=(row_spec, cache_spec, cache_spec, len_spec, full_spec, full_spec, full_spec, full_spec), out_specs=(row_spec, cache_spec, cache_spec), check_vma=False)
```

profile of v0, /device:TPU:0, one launch (start us, length us, event | category | flops | bytes accessed | tf_op | source)
XLA Modules:
  0.0 535.2 jit_solution(17625403910479857008)
XLA Ops:
  1.8 2.7 fusion.74
  5.0 15.0 %fusion.75 = f32[128,3584]{0,1:T(8,128)S(1)} fusion(bf16[128,3584]{1,0:T(8,128)(2,1)S(1)} %copy-done, bf16[3584,3584]{1,0:T(8,128)(2,1)} %param.14), kind=kOutput, calls=%fused_computation.103 | convolution fusion | flops 3288334336 | bytes 28442624 | tf_op jit(solution)/shard_map/dot_general | solution.py:63
  21.2 2.3 copy.52
  23.4 2.3 copy.53
  25.7 2.1 pad_maximum_fusion
  27.9 1.7 fusion.52
  30.3 20.7 %bitcast_reduce_fusion.1 = (f32[128,4,7]{0,2,1:T(8,128)S(1)}, f32[4,128,7,4096]{3,1,2,0:T(8,128)}) fusion(pred[4096]{0:T(1024)(128)(4,1)S(1)} %iota_compare_fusion.1, bf16[128,4,7,128]{3,0,2,1:T(8,128)(2,1)S(1)} %pad_maximum_fusion, bf16[4096,4,128,1]{2,1,0,3:T(4,128)(2,1)S(1)} %bitcast.143), kind=kOutput, calls=%fused_computation.49 | convolution fusion | flops 3802132992 | bytes 63850496 | tf_op jit(solution)/shard_map/nkgd,skd->nkgs/dot_general | solution.py:33
  51.6 25.3 %fusion.45 = f32[4,128,7,128]{3,1,2,0:T(8,128)} fusion(f32[4,128,7,4096]{3,1,2,0:T(8,128)} %get-tuple-element.474, f32[128,4,7]{0,2,1:T(8,128)} %max.38, pred[4096]{0:T(1024)(128)(4,1)S(1)} %iota_compare_fusion.1, bf16[4096,4,128,1]{2,1,0,3:T(4,128)(2,1)} %bitcast.146), kind=kOutput, calls=%fused_computation.55 | convolution fusion | flops 3831496704 | bytes 64768000 | tf_op jit(solution)/shard_map/nkgs,skd->nkgd/dot_general | solution.py:43
  78.3 3.5 bitcast_add_fusion
  83.0 19.7 %fusion.44 = f32[128,4,7]{0,2,1:T(8,128)S(1)} fusion(f32[4,128,7,4096]{3,1,2,0:T(8,128)} %get-tuple-element.474, f32[128,4,7]{0,2,1:T(8,128)} %max.38, pred[4096]{0:T(1024)(128)(4,1)S(1)} %iota_compare_fusion.1), kind=kLoop, calls=%fused_computation.54 | loop fusion | flops 73396736 | bytes 58753024 | tf_op jit(solution)/shard_map/reduce_sum | solution.py:42
  102.7 4.8 copy.59
  107.6 2.5 copy.60
  110.1 410.9 %while.32 = (s32[]{:T(128)}, bf16[4096,4,128]{2,0,1:T(8,128)(2,1)}, bf16[4096,4,128]{2,0,1:T(8,128)(2,1)}, s32[1]{0:T(128)}, bf16[128,4,128]{2,0,1:T(8,128)(2,1)...) while((s32[]{:T(128)}, bf16[4096,4,128]{2,0,1:T(8,128)(2,1)}, ...), condition=%wide.region_9.10_spmd.clone.clone, body=%wide.region_4.9_spmd.clone.clone.sunk | while | flops 7949750784 | bytes 259136048 | solution.py:87
  110.9 2.6 collective-permute-start.3
  113.5 4.4 collective-permute-start.2
  117.9 42.5 %collective-permute-start.4 = (bf16[128,4,128]{2,0,1:T(8,128)(2,1)S(1)}, bf16[128,4,128]{2,0,1:T(8,128)(2,1)S(1)}, u32[]{:S(2)}, u32[]{:S(2)}) collective-permute-start(bf16[128,4,128]{2,0,1:T(8,128)(2,1)S(1)} %get-tuple-element.588), channel_id=1, source_target_pairs={{0,1},{1,2},{2,3},{3,0},{4,5},{5,6},{6,7},{7,4}} | collective-permute-start | bytes 393224 | tf_op jit(solution)/shard_map/while/body/eval_jaxpr/ppermute | solution.py:76
  161.1 1.2 collective-permute-done.4
  162.8 23.6 %bitcast_reduce_fusion.3 = (f32[128,4,7]{0,2,1:T(8,128)S(1)}, f32[4,4096,128,7]{2,1,3,0:T(8,128)}) fusion(pred[4096]{0:T(1024)(128)(4,1)S(1)} %iota_compare_fusion.3, bf16[128,4,7,128]{3,0,2,1:T(8,128)(2,1)S(1)} %get-tuple-element.609, bf16[4096,4,128]{2,0,1:T(8,128)(2,1)} %collective-permute-done), kind=kOutput, calls=%fused_computation.2.clone.1 | convolution fusion | flops 3802132992 | bytes 63850496 | tf_op jit(solution)/shard_map/while/body/eval_jaxpr/nkgd,skd->nkgs/dot_general | solution.py:33
  186.9 4.4 copy.118
  191.3 19.4 %fusion.111 = f32[128,4,7]{0,2,1:T(8,128)S(1)} fusion(f32[4,4096,128,7]{2,1,3,0:T(8,128)} %get-tuple-element.558, f32[128,4,7]{0,2,1:T(8,128)S(1)} %max.47, pred[4096]{0:T(1024)(128)(4,1)S(1)} %iota_compare_fusion.3), kind=kLoop, calls=%fused_computation.7.clone.1 | loop fusion | flops 73396736 | bytes 58753024 | tf_op jit(solution)/shard_map/while/body/eval_jaxpr/reduce_sum | solution.py:42
  210.7 1.3 multiply_add_fusion.2
  212.0 1.9 fusion.113
  213.9 4.6 copy.119
  218.5 28.7 %fusion.114 = f32[128,4,7,128]{3,0,2,1:T(8,128)} fusion(f32[4,128,7,128]{3,1,2,0:T(8,128)S(1)} %copy-done.4, f32[128,4,7,128]{3,0,2,1:T(8,128)} %get-tuple-element.591, bf16[4096,4,128]{2,0,1:T(8,128)(2,1)} %collective-permute-done.1, f32[4,4096,128,7]{2,1,3,0:T(8,128)} %get-tuple-element.558, f32[128,4,7]{0,2,1:T(8,128)S(1)} %max.47, ...), kind=kOutput, calls=%fused_computation.15.clone.1 | convolution fusion | flops 3833331712 | bytes 68466688 | tf_op jit(solution)/shard_map/while/body/eval_jaxpr/nkgs,skd->nkgd/dot_general | solution.py:43
  247.8 2.4 collective-permute-start.3
  250.2 4.6 collective-permute-start.2
  254.8 42.3 %collective-permute-start.4 = (bf16[128,4,128]{2,0,1:T(8,128)(2,1)S(1)}, bf16[128,4,128]{2,0,1:T(8,128)(2,1)S(1)}, u32[]{:S(2)}, u32[]{:S(2)}) collective-permute-start(bf16[128,4,128]{2,0,1:T(8,128)(2,1)S(1)} %get-tuple-element.588), channel_id=1, source_target_pairs={{0,1},{1,2},{2,3},{3,0},{4,5},{5,6},{6,7},{7,4}} | collective-permute-start | bytes 393224 | tf_op jit(solution)/shard_map/while/body/eval_jaxpr/ppermute | solution.py:76
  297.8 1.2 collective-permute-done.4
  299.5 23.6 %bitcast_reduce_fusion.3 = (f32[128,4,7]{0,2,1:T(8,128)S(1)}, f32[4,4096,128,7]{2,1,3,0:T(8,128)}) fusion(pred[4096]{0:T(1024)(128)(4,1)S(1)} %iota_compare_fusion.3, bf16[128,4,7,128]{3,0,2,1:T(8,128)(2,1)S(1)} %get-tuple-element.609, bf16[4096,4,128]{2,0,1:T(8,128)(2,1)} %collective-permute-done), kind=kOutput, calls=%fused_computation.2.clone.1 | convolution fusion | flops 3802132992 | bytes 63850496 | tf_op jit(solution)/shard_map/while/body/eval_jaxpr/nkgd,skd->nkgs/dot_general | solution.py:33
  323.5 4.4 copy.118
  327.9 19.4 %fusion.111 = f32[128,4,7]{0,2,1:T(8,128)S(1)} fusion(f32[4,4096,128,7]{2,1,3,0:T(8,128)} %get-tuple-element.558, f32[128,4,7]{0,2,1:T(8,128)S(1)} %max.47, pred[4096]{0:T(1024)(128)(4,1)S(1)} %iota_compare_fusion.3), kind=kLoop, calls=%fused_computation.7.clone.1 | loop fusion | flops 73396736 | bytes 58753024 | tf_op jit(solution)/shard_map/while/body/eval_jaxpr/reduce_sum | solution.py:42
  347.3 1.3 multiply_add_fusion.2
  348.7 1.9 fusion.113
  350.6 4.6 copy.119
  355.2 28.7 %fusion.114 = f32[128,4,7,128]{3,0,2,1:T(8,128)} fusion(f32[4,128,7,128]{3,1,2,0:T(8,128)S(1)} %copy-done.4, f32[128,4,7,128]{3,0,2,1:T(8,128)} %get-tuple-element.591, bf16[4096,4,128]{2,0,1:T(8,128)(2,1)} %collective-permute-done.1, f32[4,4096,128,7]{2,1,3,0:T(8,128)} %get-tuple-element.558, f32[128,4,7]{0,2,1:T(8,128)S(1)} %max.47, ...), kind=kOutput, calls=%fused_computation.15.clone.1 | convolution fusion | flops 3833331712 | bytes 68466688 | tf_op jit(solution)/shard_map/while/body/eval_jaxpr/nkgs,skd->nkgd/dot_general | solution.py:43
  384.4 2.4 collective-permute-start.3
  386.8 4.6 collective-permute-start.2
  391.4 42.3 %collective-permute-start.4 = (bf16[128,4,128]{2,0,1:T(8,128)(2,1)S(1)}, bf16[128,4,128]{2,0,1:T(8,128)(2,1)S(1)}, u32[]{:S(2)}, u32[]{:S(2)}) collective-permute-start(bf16[128,4,128]{2,0,1:T(8,128)(2,1)S(1)} %get-tuple-element.588), channel_id=1, source_target_pairs={{0,1},{1,2},{2,3},{3,0},{4,5},{5,6},{6,7},{7,4}} | collective-permute-start | bytes 393224 | tf_op jit(solution)/shard_map/while/body/eval_jaxpr/ppermute | solution.py:76
  434.4 1.2 collective-permute-done.4
  436.1 23.6 %bitcast_reduce_fusion.3 = (f32[128,4,7]{0,2,1:T(8,128)S(1)}, f32[4,4096,128,7]{2,1,3,0:T(8,128)}) fusion(pred[4096]{0:T(1024)(128)(4,1)S(1)} %iota_compare_fusion.3, bf16[128,4,7,128]{3,0,2,1:T(8,128)(2,1)S(1)} %get-tuple-element.609, bf16[4096,4,128]{2,0,1:T(8,128)(2,1)} %collective-permute-done), kind=kOutput, calls=%fused_computation.2.clone.1 | convolution fusion | flops 3802132992 | bytes 63850496 | tf_op jit(solution)/shard_map/while/body/eval_jaxpr/nkgd,skd->nkgs/dot_general | solution.py:33
  460.2 4.4 copy.118
  464.6 19.4 %fusion.111 = f32[128,4,7]{0,2,1:T(8,128)S(1)} fusion(f32[4,4096,128,7]{2,1,3,0:T(8,128)} %get-tuple-element.558, f32[128,4,7]{0,2,1:T(8,128)S(1)} %max.47, pred[4096]{0:T(1024)(128)(4,1)S(1)} %iota_compare_fusion.3), kind=kLoop, calls=%fused_computation.7.clone.1 | loop fusion | flops 73396736 | bytes 58753024 | tf_op jit(solution)/shard_map/while/body/eval_jaxpr/reduce_sum | solution.py:42
  484.0 1.3 multiply_add_fusion.2
  485.3 1.9 fusion.113
  487.2 4.6 copy.119
  491.8 28.7 %fusion.114 = f32[128,4,7,128]{3,0,2,1:T(8,128)} fusion(f32[4,128,7,128]{3,1,2,0:T(8,128)S(1)} %copy-done.4, f32[128,4,7,128]{3,0,2,1:T(8,128)} %get-tuple-element.591, bf16[4096,4,128]{2,0,1:T(8,128)(2,1)} %collective-permute-done.1, f32[4,4096,128,7]{2,1,3,0:T(8,128)} %get-tuple-element.558, f32[128,4,7]{0,2,1:T(8,128)S(1)} %max.47, ...), kind=kOutput, calls=%fused_computation.15.clone.1 | convolution fusion | flops 3833331712 | bytes 68466688 | tf_op jit(solution)/shard_map/while/body/eval_jaxpr/nkgs,skd->nkgd/dot_general | solution.py:43
  521.0 1.8 copy.62
  523.1 11.3 %convolution_convert_fusion = bf16[128,3584]{1,0:T(8,128)(2,1)} fusion(bf16[128,3584]{0,1:T(8,128)(2,1)S(1)} %bitcast.145, bf16[3584,3584]{1,0:T(8,128)(2,1)} %param.17), kind=kOutput, calls=%fused_computation.58 | convolution fusion | flops 3288793088 | bytes 27525120 | tf_op jit(solution)/shard_map/dot_general | solution.py:89
  (95 shorter events, 13.0 us)
Async XLA Ops:
  0.6 1.2 copy-start
  5.0 97.7 %copy-start.9 = (bf16[128,4,128]{2,0,1:T(8,128)(2,1)}, bf16[128,4,128]{2,0,1:T(8,128)(2,1)S(1)}, u32[]{:S(2)}) copy-start(bf16[128,4,128]{2,0,1:T(8,128)(2,1)S(1)} %pad_maximum_fusion.1) | copy-start | bytes 393220
  25.7 4.6 copy-start.5
  27.8 23.1 %copy-start.2 = (bf16[128,4,7,128]{3,0,2,1:T(8,128)(2,1)}, bf16[128,4,7,128]{3,0,2,1:T(8,128)(2,1)S(1)}, u32[]{:S(2)}) copy-start(bf16[128,4,7,128]{3,0,2,1:T(8,128)(2,1)S(1)} %pad_maximum_fusion) | copy-start | bytes 2752516
  51.5 25.3 %copy-start.8 = (bf16[3584,512]{1,0:T(8,128)(2,1)S(1)}, bf16[3584,512]{1,0:T(8,128)(2,1)}, u32[]{:S(2)}) copy-start(bf16[3584,512]{1,0:T(8,128)(2,1)} %param.16) | copy-start | bytes 11010052
  76.8 1.5 copy-start.6
  77.5 25.1 %copy-start.12 = (bf16[128,4,128]{2,1,0:T(4,128)(2,1)}, bf16[128,4,128]{2,1,0:T(4,128)(2,1)S(1)}, u32[]{:S(2)}) copy-start(bf16[128,4,128]{2,1,0:T(4,128)(2,1)S(1)} %reshape.199) | copy-start | bytes 393220
  102.7 4.8 copy-start.7
  107.6 2.5 copy-start.3
  107.6 2.5 copy-start.11
  110.1 52.8 %collective-permute-start = (bf16[4096,4,128]{2,0,1:T(8,128)(2,1)}, bf16[4096,4,128]{2,0,1:T(8,128)(2,1)}, u32[]{:S(2)}, u32[]{:S(2)}) collective-permute-start(bf16[4096,4,128]{2,0,1:T(8,128)(2,1)} %get-tuple-element.584), channel_id=1, source_target_pairs={{0,1},{1,2},{2,3},{3,0},{4,5},{5,6},{6,7},{7,4}} | collective-permute-start | bytes 12582920 | tf_op jit(solution)/shard_map/while/body/eval_jaxpr/ppermute | solution.py:72
  110.9 50.1 %collective-permute-start.3 = (bf16[128,4,128]{2,0,1:T(8,128)(2,1)S(1)}, bf16[128,4,128]{2,0,1:T(8,128)(2,1)S(1)}, u32[]{:S(2)}, u32[]{:S(2)}) collective-permute-start(bf16[128,4,128]{2,0,1:T(8,128)(2,1)S(1)} %get-tuple-element.587), channel_id=1, source_target_pairs={{0,1},{1,2},{2,3},{3,0},{4,5},{5,6},{6,7},{7,4}} | collective-permute-start | bytes 393224 | tf_op jit(solution)/shard_map/while/body/eval_jaxpr/ppermute | solution.py:75
  113.5 47.0 %collective-permute-start.2 = (s32[1]{0:T(128)}, s32[1]{0:T(128)}, u32[]{:S(2)}, u32[]{:S(2)}) collective-permute-start(s32[1]{0:T(128)} %copy.111), channel_id=1, source_target_pairs={{0,1},{1,2},{2,3},{3,0},{4,5},{5,6},{6,7},{7,4}} | collective-permute-start | bytes 20 | tf_op jit(solution)/shard_map/while/body/eval_jaxpr/ppermute | solution.py:74
  117.9 44.4 %collective-permute-start.4 = (bf16[128,4,128]{2,0,1:T(8,128)(2,1)S(1)}, bf16[128,4,128]{2,0,1:T(8,128)(2,1)S(1)}, u32[]{:S(2)}, u32[]{:S(2)}) collective-permute-start(bf16[128,4,128]{2,0,1:T(8,128)(2,1)S(1)} %get-tuple-element.588), channel_id=1, source_target_pairs={{0,1},{1,2},{2,3},{3,0},{4,5},{5,6},{6,7},{7,4}} | collective-permute-start | bytes 393224 | tf_op jit(solution)/shard_map/while/body/eval_jaxpr/ppermute | solution.py:76
  160.4 53.5 %collective-permute-start.1 = (bf16[4096,4,128]{2,0,1:T(8,128)(2,1)}, bf16[4096,4,128]{2,0,1:T(8,128)(2,1)}, u32[]{:S(2)}, u32[]{:S(2)}) collective-permute-start(bf16[4096,4,128]{2,0,1:T(8,128)(2,1)} %get-tuple-element.585), channel_id=1, source_target_pairs={{0,1},{1,2},{2,3},{3,0},{4,5},{5,6},{6,7},{7,4}} | collective-permute-start | bytes 12582920 | tf_op jit(solution)/shard_map/while/body/eval_jaxpr/ppermute | solution.py:73
  213.9 4.6 copy-start.4
  247.7 51.7 %collective-permute-start = (bf16[4096,4,128]{2,0,1:T(8,128)(2,1)}, bf16[4096,4,128]{2,0,1:T(8,128)(2,1)}, u32[]{:S(2)}, u32[]{:S(2)}) collective-permute-start(bf16[4096,4,128]{2,0,1:T(8,128)(2,1)} %get-tuple-element.584), channel_id=1, source_target_pairs={{0,1},{1,2},{2,3},{3,0},{4,5},{5,6},{6,7},{7,4}} | collective-permute-start | bytes 12582920 | tf_op jit(solution)/shard_map/while/body/eval_jaxpr/ppermute | solution.py:72
  247.8 50.0 %collective-permute-start.3 = (bf16[128,4,128]{2,0,1:T(8,128)(2,1)S(1)}, bf16[128,4,128]{2,0,1:T(8,128)(2,1)S(1)}, u32[]{:S(2)}, u32[]{:S(2)}) collective-permute-start(bf16[128,4,128]{2,0,1:T(8,128)(2,1)S(1)} %get-tuple-element.587), channel_id=1, source_target_pairs={{0,1},{1,2},{2,3},{3,0},{4,5},{5,6},{6,7},{7,4}} | collective-permute-start | bytes 393224 | tf_op jit(solution)/shard_map/while/body/eval_jaxpr/ppermute | solution.py:75
  250.2 47.0 %collective-permute-start.2 = (s32[1]{0:T(128)}, s32[1]{0:T(128)}, u32[]{:S(2)}, u32[]{:S(2)}) collective-permute-start(s32[1]{0:T(128)} %copy.111), channel_id=1, source_target_pairs={{0,1},{1,2},{2,3},{3,0},{4,5},{5,6},{6,7},{7,4}} | collective-permute-start | bytes 20 | tf_op jit(solution)/shard_map/while/body/eval_jaxpr/ppermute | solution.py:74
  254.8 44.3 %collective-permute-start.4 = (bf16[128,4,128]{2,0,1:T(8,128)(2,1)S(1)}, bf16[128,4,128]{2,0,1:T(8,128)(2,1)S(1)}, u32[]{:S(2)}, u32[]{:S(2)}) collective-permute-start(bf16[128,4,128]{2,0,1:T(8,128)(2,1)S(1)} %get-tuple-element.588), channel_id=1, source_target_pairs={{0,1},{1,2},{2,3},{3,0},{4,5},{5,6},{6,7},{7,4}} | collective-permute-start | bytes 393224 | tf_op jit(solution)/shard_map/while/body/eval_jaxpr/ppermute | solution.py:76
  297.0 53.5 %collective-permute-start.1 = (bf16[4096,4,128]{2,0,1:T(8,128)(2,1)}, bf16[4096,4,128]{2,0,1:T(8,128)(2,1)}, u32[]{:S(2)}, u32[]{:S(2)}) collective-permute-start(bf16[4096,4,128]{2,0,1:T(8,128)(2,1)} %get-tuple-element.585), channel_id=1, source_target_pairs={{0,1},{1,2},{2,3},{3,0},{4,5},{5,6},{6,7},{7,4}} | collective-permute-start | bytes 12582920 | tf_op jit(solution)/shard_map/while/body/eval_jaxpr/ppermute | solution.py:73
  350.6 4.6 copy-start.4
  384.4 51.7 %collective-permute-start = (bf16[4096,4,128]{2,0,1:T(8,128)(2,1)}, bf16[4096,4,128]{2,0,1:T(8,128)(2,1)}, u32[]{:S(2)}, u32[]{:S(2)}) collective-permute-start(bf16[4096,4,128]{2,0,1:T(8,128)(2,1)} %get-tuple-element.584), channel_id=1, source_target_pairs={{0,1},{1,2},{2,3},{3,0},{4,5},{5,6},{6,7},{7,4}} | collective-permute-start | bytes 12582920 | tf_op jit(solution)/shard_map/while/body/eval_jaxpr/ppermute | solution.py:72
  384.4 50.0 %collective-permute-start.3 = (bf16[128,4,128]{2,0,1:T(8,128)(2,1)S(1)}, bf16[128,4,128]{2,0,1:T(8,128)(2,1)S(1)}, u32[]{:S(2)}, u32[]{:S(2)}) collective-permute-start(bf16[128,4,128]{2,0,1:T(8,128)(2,1)S(1)} %get-tuple-element.587), channel_id=1, source_target_pairs={{0,1},{1,2},{2,3},{3,0},{4,5},{5,6},{6,7},{7,4}} | collective-permute-start | bytes 393224 | tf_op jit(solution)/shard_map/while/body/eval_jaxpr/ppermute | solution.py:75
  386.8 47.0 %collective-permute-start.2 = (s32[1]{0:T(128)}, s32[1]{0:T(128)}, u32[]{:S(2)}, u32[]{:S(2)}) collective-permute-start(s32[1]{0:T(128)} %copy.111), channel_id=1, source_target_pairs={{0,1},{1,2},{2,3},{3,0},{4,5},{5,6},{6,7},{7,4}} | collective-permute-start | bytes 20 | tf_op jit(solution)/shard_map/while/body/eval_jaxpr/ppermute | solution.py:74
  391.4 44.3 %collective-permute-start.4 = (bf16[128,4,128]{2,0,1:T(8,128)(2,1)S(1)}, bf16[128,4,128]{2,0,1:T(8,128)(2,1)S(1)}, u32[]{:S(2)}, u32[]{:S(2)}) collective-permute-start(bf16[128,4,128]{2,0,1:T(8,128)(2,1)S(1)} %get-tuple-element.588), channel_id=1, source_target_pairs={{0,1},{1,2},{2,3},{3,0},{4,5},{5,6},{6,7},{7,4}} | collective-permute-start | bytes 393224 | tf_op jit(solution)/shard_map/while/body/eval_jaxpr/ppermute | solution.py:76
  433.7 53.5 %collective-permute-start.1 = (bf16[4096,4,128]{2,0,1:T(8,128)(2,1)}, bf16[4096,4,128]{2,0,1:T(8,128)(2,1)}, u32[]{:S(2)}, u32[]{:S(2)}) collective-permute-start(bf16[4096,4,128]{2,0,1:T(8,128)(2,1)} %get-tuple-element.585), channel_id=1, source_target_pairs={{0,1},{1,2},{2,3},{3,0},{4,5},{5,6},{6,7},{7,4}} | collective-permute-start | bytes 12582920 | tf_op jit(solution)/shard_map/while/body/eval_jaxpr/ppermute | solution.py:73
  487.2 4.6 copy-start.4
  523.1 11.3 %copy-start.10 = (bf16[128,4,128]{2,0,1:T(8,128)(2,1)S(1)}, bf16[128,4,128]{2,0,1:T(8,128)(2,1)}, u32[]{:S(2)}) copy-start(bf16[128,4,128]{2,0,1:T(8,128)(2,1)} %copy-done.9) | copy-start | bytes 393220
  523.1 12.1 %copy-start.1 = (bf16[128,3584]{1,0:T(8,128)(2,1)S(1)}, bf16[128,3584]{1,0:T(8,128)(2,1)}, u32[]{:S(2)}) copy-start(bf16[128,3584]{1,0:T(8,128)(2,1)} %param.10) | copy-start | bytes 2752516
where the time goes:
time: 536 us; the launch traced here: 535 us
  matrix products  244 us (46%)
  starting transfers between devices  149 us (28%)
  other arithmetic  91.1 us (17%)
  local copies, waits for them, and re-layouts  43.5 us (8%)
    ppermute x3, starting transfers between devices, visit_step(): v_seg = lax.ppermute(v_seg, 'cp', shift_perm)  127 us
    dot_general x4, matrix products, block_attend(): jnp.einsum('nkgs,skd->nkgd', ctx_wt.astype(jnp.bfloat16), v_ctx, preferre...  111 us
    dot_general x4, matrix products, block_attend(): jnp.einsum('nkgd,skd->nkgs', q_blk, k_ctx, preferred_element_type=jnp.flo...  91.4 us
    reduce_sum x8, other arithmetic, block_attend(): blk_sum = ctx_wt.sum(axis=-1) + seg_wt.sum(axis=-1)  80.4 us
    while x18, local copies, waits for them, and re-layouts  27 us
    dot_general x1, matrix products, device_fn(): jnp.dot(x_new, w_q, preferred_element_type=jnp.float32)  15 us
    ppermute x3, starting transfers between devices, visit_step(): ctx_len = lax.ppermute(ctx_len, 'cp', shift_perm)  13.5 us
    dot_general x1, matrix products, device_fn(): jnp.dot(attention, w_o, preferred_element_type=jnp.float32)  11.3 us
  transfers between devices with their start and end apart: 15, of which 3 were waited for; matrix products, arithmetic and copies ran while one was open for 29% of the time, Pallas kernels for 0%

commit v1 on v0

v1 whole, which is shorter than its diff:
```python
import functools
import math

import jax
import jax.numpy as jnp
import numpy as np
from jax import lax
from jax.experimental import pallas as pl
from jax.experimental.pallas import tpu as pltpu
from jax.sharding import PartitionSpec as P

ROPE_BASE = 500000.0
MESH = pl.DeviceIdType.MESH
KEY_TILE = 1024
PREP = 128
HIDE = -3e38


def rope_constants(tok_dev, cp_size, cache_len, head_dim):
    piece = tok_dev // 2
    half = head_dim // 2
    inv_freq = ROPE_BASE ** (-np.arange(half, dtype=np.float64) * 2.0 / head_dim)
    within = np.arange(tok_dev)
    rows = []
    for dev in range(cp_size):
        piece_ids = np.where(within < piece, dev, 2 * cp_size - 1 - dev)
        rows.append(cache_len + piece_ids * piece + within % piece)
    angles = np.concatenate(rows).astype(np.float64)[:, None] * inv_freq[None, :]
    cos, sin = np.cos(angles), np.sin(angles)
    cos_full = np.concatenate([cos, cos], axis=1).astype(np.float32)
    sin_full = np.concatenate([-sin, sin], axis=1).astype(np.float32)
    shape = (cp_size // 2, 2 * tok_dev, head_dim)
    return cos_full.reshape(shape), sin_full.reshape(shape)


def dot_t(lhs, rhs):
    return lax.dot_general(lhs, rhs, (((1,), (1,)), ((), ())), preferred_element_type=jnp.float32)


def kernel(dims, len_ref, x_ref, k_ref, v_ref, wq_ref, wk_ref, wv_ref, wo_ref, cos_ref, sin_ref, y_ref, ko_ref, vo_ref,
           xbuf, raw_k, raw_v, lens, kb, vt, kn, vtn, wbuf, wo1, cosb, sinb, qbuf, ob, pb, oall, ost, kvx,
           loc_sem, wq_sem, pair_s, pair_r, q_s, q_r, p_s, p_r, o_s, o_r):
    heads, head_dim, group, tok, cache, cp_size = dims
    my_heads = heads // 2
    half_cols = my_heads * head_dim
    toks = 2 * tok
    pair = 2 * head_dim
    score_c = math.log2(math.e) / math.sqrt(head_dim)

    me = lax.axis_index('cp')
    core = lax.rem(me, 2)
    chip = lax.div(me, 2)
    mate = me + 1 - 2 * core
    peer = lax.rem(me + 2, cp_size)

    def remote(src, dst, send, recv, dev):
        return pltpu.make_async_remote_copy(src_ref=src, dst_ref=dst, send_sem=send, recv_sem=recv, device_id={'cp': dev}, device_id_type=MESH)

    ld_x = pltpu.make_async_copy(x_ref, xbuf.at[pl.ds(pl.multiple_of(core * tok, tok), tok)], loc_sem.at[0])
    ld_cos = pltpu.make_async_copy(cos_ref.at[chip], cosb, loc_sem.at[1])
    ld_sin = pltpu.make_async_copy(sin_ref.at[chip], sinb, loc_sem.at[2])
    ld_k = pltpu.make_async_copy(k_ref.at[:, core], raw_k.at[0], loc_sem.at[3])
    ld_v = pltpu.make_async_copy(v_ref.at[:, core], raw_v.at[0], loc_sem.at[4])
    n_chunk = my_heads // 2

    def ld_wq(j):
        col = pl.multiple_of(core * half_cols + j * pair, pair)
        return pltpu.make_async_copy(wq_ref.at[:, pl.ds(col, pair)], wbuf.at[:, pl.ds(pl.multiple_of(j * pair, pair), pair)], wq_sem.at[j])

    kv_col = pl.multiple_of(core * pair, pair)
    ld_wk = pltpu.make_async_copy(wk_ref.at[:, pl.ds(kv_col, pair)], wo1.at[:, pl.ds(0, pair)], loc_sem.at[5])
    ld_wv = pltpu.make_async_copy(wv_ref.at[:, pl.ds(kv_col, pair)], wo1.at[:, pl.ds(pair, pair)], loc_sem.at[6])
    ld_wo0 = pltpu.make_async_copy(wo_ref.at[:, pl.ds(0, half_cols)], wbuf, loc_sem.at[7])
    ld_wo1 = pltpu.make_async_copy(wo_ref.at[:, pl.ds(half_cols, half_cols)], wo1, loc_sem.at[8])
    ld_x.start()
    ld_wq(0).start()
    ld_cos.start()
    ld_sin.start()
    lens[0] = jnp.full(lens.shape[1:], len_ref[0], jnp.int32)

    barrier = pltpu.get_barrier_semaphore()
    for other in (mate, peer):
        pl.semaphore_signal(barrier, inc=1, device_id={'cp': other}, device_id_type=MESH)
    pl.semaphore_wait(barrier, 2)

    my_rows = pl.ds(pl.multiple_of(core * tok, tok), tok)
    mate_rows = pl.ds(pl.multiple_of((1 - core) * tok, tok), tok)
    cp_x = remote(x_ref, xbuf.at[my_rows], pair_s.at[0], pair_r.at[0], mate)
    cp_len = remote(lens.at[0], lens.at[1], pair_s.at[1], pair_r.at[1], mate)
    cp_k = remote(k_ref.at[:, 1 - core], raw_k.at[1], pair_s.at[2], pair_r.at[2], mate)
    cp_v = remote(v_ref.at[:, 1 - core], raw_v.at[1], pair_s.at[3], pair_r.at[3], mate)
    cp_x.start()
    for j in range(1, n_chunk):
        ld_wq(j).start()
    cp_len.start()
    cp_k.start()
    cp_v.start()
    ld_wk.start()
    ld_wv.start()
    ld_k.start()
    ld_v.start()

    def rope(vals):
        return vals * cosb[...] + pltpu.roll(vals, head_dim // 2, 1) * sinb[...]

    def cp_q(j):
        src = qbuf.at[pl.ds(2 * j, 2)]
        return remote(src, qbuf.at[pl.ds(my_heads + 2 * j, 2)], q_s.at[j], q_r.at[j], peer)

    ld_x.wait()
    ld_cos.wait()
    ld_sin.wait()
    cp_x.wait_recv()

    def q_step(j, carry):
        ld_wq(j).wait()
        proj = jnp.dot(xbuf[...], wbuf[:, pl.ds(pl.multiple_of(j * pair, pair), pair)], preferred_element_type=jnp.float32)
        qbuf[2 * j] = rope(proj[:, :head_dim]).astype(jnp.bfloat16)
        qbuf[2 * j + 1] = rope(proj[:, head_dim:]).astype(jnp.bfloat16)
        cp_q(j).start()
        return carry

    lax.fori_loop(0, n_chunk, q_step, 0)
    ld_wo0.start()

    ld_wk.wait()
    ld_wv.wait()
    k_proj = jnp.dot(xbuf[...], wo1[:, :pair], preferred_element_type=jnp.float32)
    v_proj = jnp.dot(xbuf[...], wo1[:, pair:2 * pair], preferred_element_type=jnp.float32)
    for h in range(2):
        kn[h] = rope(k_proj[:, h * head_dim:(h + 1) * head_dim]).astype(jnp.bfloat16)
        v_h = v_proj[:, h * head_dim:(h + 1) * head_dim].astype(jnp.bfloat16)
        vtn[h] = v_proj[:, h * head_dim:(h + 1) * head_dim].T.astype(jnp.bfloat16)
        kvx[0, :, h * head_dim:(h + 1) * head_dim] = kn[h]
        kvx[1, :, h * head_dim:(h + 1) * head_dim] = v_h
    ld_wo1.start()
    cp_ko = remote(kvx.at[0, mate_rows], kvx.at[2, pl.ds(0, tok)], pair_s.at[4], pair_r.at[4], mate)
    cp_vo = remote(kvx.at[1, mate_rows], kvx.at[2, pl.ds(tok, tok)], pair_s.at[5], pair_r.at[5], mate)
    cp_ko.start()
    cp_vo.start()

    row = lax.broadcasted_iota(jnp.int32, (2 * PREP, 2 * PREP), 0)
    col = lax.broadcasted_iota(jnp.int32, (2 * PREP, 2 * PREP), 1)
    want = jnp.where(row < PREP, 2 * row, 2 * (row - PREP) + 1)
    pick = jnp.where(col == want, 1.0, 0.0).astype(jnp.bfloat16)
    lane = lax.broadcasted_iota(jnp.int32, (PREP, head_dim), 1)
    slot = lax.broadcasted_iota(jnp.int32, (PREP, head_dim), 0)

    def prep(block):
        def step(i, carry):
            at = pl.multiple_of(i * PREP, PREP)
            to = pl.multiple_of(block * cache + i * PREP, PREP)
            both = jnp.concatenate([raw_k[block, pl.ds(at, PREP)].reshape(2 * PREP, head_dim), raw_v[block, pl.ds(at, PREP)].reshape(2 * PREP, head_dim)], axis=1)
            split = jnp.dot(pick, both, preferred_element_type=jnp.float32)
            hidden = jnp.where((slot + at >= lens[block, 0:1, :]) & (lane == 0), HIDE, 0.0).astype(jnp.bfloat16)
            for h in range(2):
                part = split[h * PREP:(h + 1) * PREP]
                kb[h, pl.ds(to, PREP), :head_dim] = part[:, :head_dim].astype(jnp.bfloat16)
                kb[h, pl.ds(to, PREP), head_dim:] = hidden
                vt[h, :, pl.ds(to, PREP)] = part[:, head_dim:].T.astype(jnp.bfloat16)
            return carry

        lax.fori_loop(0, cache // PREP, step, 0)

    ld_k.wait()
    ld_v.wait()
    prep(0)
    cp_len.wait_recv()
    cp_k.wait_recv()
    cp_v.wait_recv()
    prep(1)

    n_tiles = 2 * cache // KEY_TILE
    first_a = 2
    ones_col = jnp.where(lax.broadcasted_iota(jnp.int32, (toks, head_dim), 1) == 0, 1.0, 0.0).astype(jnp.bfloat16)

    def positions(chip_id, axis):
        within = lax.broadcasted_iota(jnp.int32, (toks, toks), axis)
        dev = 2 * chip_id + jnp.where(within >= tok, 1, 0)
        inner = jnp.where(within >= tok, within - tok, within)
        late = inner >= tok // 2
        piece_id = jnp.where(late, 2 * cp_size - 1 - dev, dev)
        return piece_id * (tok // 2) + jnp.where(late, inner - tok // 2, inner)

    def cp_p(h):
        return remote(ob.at[my_heads + h], pb.at[h], p_s.at[h], p_r.at[h], peer)

    def attend(i, carry):
        is_b = jnp.logical_and(i >= first_a, i < first_a + my_heads)
        idx = jnp.where(i < first_a, i, jnp.where(is_b, my_heads + i - first_a, i - my_heads))
        head = jnp.where(is_b, idx - my_heads, idx)
        kvh = lax.div(head, group)
        q_chip = jnp.where(is_b, 1 - chip, chip)

        @pl.when(jnp.logical_and(is_b, lax.rem(head, 2) == 0))
        def _():
            cp_q(lax.div(head, 2)).wait_recv()

        q = qbuf[idx]
        q_aug = jnp.concatenate([q, ones_col], axis=1)
        top = None
        for t in range(n_tiles + 1):
            if t < n_tiles:
                s = dot_t(kb[kvh, t * KEY_TILE:(t + 1) * KEY_TILE], q_aug)
                vals = vt[kvh, :, t * KEY_TILE:(t + 1) * KEY_TILE]
            else:
                s = dot_t(kn[kvh], q)
                s = jnp.where(positions(chip, 0) <= positions(q_chip, 1), s, -jnp.inf)
                vals = vtn[kvh]
            tile_top = jnp.max(s, axis=0, keepdims=True)
            new_top = tile_top if top is None else jnp.maximum(top, tile_top)
            w = jnp.exp2((s - new_top) * score_c)
            w_sum = jnp.sum(w, axis=0, keepdims=True)
            out = jnp.dot(vals, w.astype(jnp.bfloat16), preferred_element_type=jnp.float32)
            if top is None:
                total, acc = w_sum, out
            else:
                keep = jnp.exp2((top - new_top) * score_c)
                total = total * keep + w_sum
                acc = acc * keep + out
            top = new_top
        ob[idx, :head_dim] = acc
        ob[idx, head_dim:head_dim + 8] = jnp.broadcast_to(top, (8, toks))
        ob[idx, head_dim + 8:head_dim + 16] = jnp.broadcast_to(total, (8, toks))

        @pl.when(is_b)
        def _():
            cp_p(head).start()

        return carry

    lax.fori_loop(0, 2 * my_heads, attend, 0)

    cp_ko.wait()
    cp_vo.wait()
    for out_ref, n in ((ko_ref, 0), (vo_ref, 1)):
        out_ref[:, pl.ds(pl.multiple_of(core * pair, pair), pair)] = kvx[n, my_rows]
        out_ref[:, pl.ds(pl.multiple_of((1 - core) * pair, pair), pair)] = kvx[2, n * tok:(n + 1) * tok]

    def cp_o(h):
        col = pl.multiple_of((core * my_heads + h) * head_dim, head_dim)
        return remote(ost.at[h, mate_rows], oall.at[:, pl.ds(col, head_dim)], o_s.at[h], o_r.at[h], mate)

    def combine(h, carry):
        cp_p(h).wait_recv()
        top_a, top_b = ob[h, head_dim:head_dim + 1], pb[h, head_dim:head_dim + 1]
        top = jnp.maximum(top_a, top_b)
        keep_a = jnp.exp2((top_a - top) * score_c)
        keep_b = jnp.exp2((top_b - top) * score_c)
        total = ob[h, head_dim + 8:head_dim + 9] * keep_a + pb[h, head_dim + 8:head_dim + 9] * keep_b
        out = (ob[h, :head_dim] * keep_a + pb[h, :head_dim] * keep_b) / total
        ost[h] = out.T.astype(jnp.bfloat16)
        cp_o(h).start()
        col = pl.multiple_of((core * my_heads + h) * head_dim, head_dim)
        oall[:, pl.ds(col, head_dim)] = ost[h, my_rows]
        return carry

    lax.fori_loop(0, my_heads, combine, 0)
    ld_wo0.wait()
    ld_wo1.wait()

    def drain(h, carry):
        cp_o(h).wait()
        cp_p(h).wait_send()
        return carry

    lax.fori_loop(0, my_heads, drain, 0)
    for half, weights in ((0, wbuf), (1, wo1)):
        for n in range(half_cols // pair):
            part = jnp.dot(oall[...], weights[:, n * pair:(n + 1) * pair], preferred_element_type=jnp.float32)
            y_ref[:, half * half_cols + n * pair:half * half_cols + (n + 1) * pair] = part.astype(jnp.bfloat16)

    for j in range(n_chunk):
        cp_q(j).wait_send()
    for copy in (cp_x, cp_len, cp_k, cp_v):
        copy.wait_send()


def solution(mesh):
    cp_size = mesh.shape['cp']
    row_spec = P(('dp', 'cp'), None)
    cache_spec = P(('dp', 'cp'), None, None)
    len_spec = P(('dp', 'cp'))
    full_spec = P()

    def device_fn(x_new, k_cache, v_cache, valid_len, w_q, w_k, w_v, w_o):
        tok, width = x_new.shape
        cache, kv_heads, head_dim = k_cache.shape
        heads = w_q.shape[1] // head_dim
        my_heads = heads // 2
        toks = 2 * tok
        half_cols = my_heads * head_dim
        cos, sin = rope_constants(tok, cp_size, cache * cp_size, head_dim)
        dims = (heads, head_dim, heads // kv_heads, tok, cache, cp_size)
        bf16, f32 = jnp.bfloat16, jnp.float32
        k4 = k_cache.reshape(cache, 2, 2, head_dim)
        v4 = v_cache.reshape(cache, 2, 2, head_dim)
        any_spec = pl.BlockSpec(memory_space=pl.ANY)
        vmem_spec = pl.BlockSpec(memory_space=pltpu.VMEM)
        dma = pltpu.SemaphoreType.DMA
        y_out, k_new, v_new = pl.pallas_call(
            functools.partial(kernel, dims),
            out_shape=(
                jax.ShapeDtypeStruct((tok, width), bf16),
                jax.ShapeDtypeStruct((tok, kv_heads * head_dim), bf16),
                jax.ShapeDtypeStruct((tok, kv_heads * head_dim), bf16),
            ),
            in_specs=[pl.BlockSpec(memory_space=pltpu.SMEM)] + [any_spec] * 9,
            out_specs=(vmem_spec,) * 3,
            scratch_shapes=[
                pltpu.VMEM((toks, width), bf16),
                pltpu.VMEM((2, cache, 2, head_dim), bf16),
                pltpu.VMEM((2, cache, 2, head_dim), bf16),
                pltpu.VMEM((2, 8, head_dim), jnp.int32),
                pltpu.VMEM((2, 2 * cache, 2 * head_dim), bf16),
                pltpu.VMEM((2, head_dim, 2 * cache), bf16),
                pltpu.VMEM((2, toks, head_dim), bf16),
                pltpu.VMEM((2, head_dim, toks), bf16),
                pltpu.VMEM((width, half_cols), bf16),
                pltpu.VMEM((width, half_cols), bf16),
                pltpu.VMEM((toks, head_dim), f32),
                pltpu.VMEM((toks, head_dim), f32),
                pltpu.VMEM((heads, toks, head_dim), bf16),
                pltpu.VMEM((heads, head_dim + 16, toks), f32),
                pltpu.VMEM((my_heads, head_dim + 16, toks), f32),
                pltpu.VMEM((tok, heads * head_dim), bf16),
                pltpu.VMEM((my_heads, toks, head_dim), bf16),
                pltpu.VMEM((3, toks, 2 * head_dim), bf16),
                dma((9,)), dma((my_heads // 2,)), dma((6,)), dma((6,)),
                dma((my_heads // 2,)), dma((my_heads // 2,)),
                dma((my_heads,)), dma((my_heads,)), dma((my_heads,)), dma((my_heads,)),
            ],
            compiler_params=pltpu.CompilerParams(collective_id=0, has_side_effects=True, vmem_limit_bytes=67043328),
        )(valid_len, x_new, k4, v4, w_q, w_k, w_v, w_o, jnp.asarray(cos), jnp.asarray(sin))
        shape = (tok, kv_heads, head_dim)
        return y_out, k_new.reshape(shape), v_new.reshape(shape)

    return jax.shard_map(device_fn, mesh=mesh, in_specs=(row_spec, cache_spec, cache_spec, len_spec, full_spec, full_spec, full_spec, full_spec), out_specs=(row_spec, cache_spec, cache_spec), check_vma=False)
```

time: 536 us -> 190 us (0.35)
  matrix products: 244 us -> 0 us
  Pallas kernels: 0 us -> 183 us
  starting transfers between devices: 149 us -> 0 us
  other arithmetic: 91.1 us -> 0 us
  local copies, waits for them, and re-layouts: 43.5 us -> 5.35 us
    dot_general x20 -> x0, matrix products: 244 us -> none  [the longest x4 111 us: block_attend(): jnp.einsum('nkgs,skd->nkgd', ctx_wt.astype(jnp.bfloat16), v_ctx, preferre...]
    pallas_call x0 -> x1, Pallas kernels: none -> 183 us  [device_fn(): pl.pallas_call(functools.partial(kernel, dims), out_shape=(jax.ShapeDtype...]
    ppermute x15 -> x0, starting transfers between devices: 149 us -> none  [the longest x3 127 us: visit_step(): v_seg = lax.ppermute(v_seg, 'cp', shift_perm)]
    reduce_sum x8 -> x0, other arithmetic: 80.4 us -> none  [block_attend(): blk_sum = ctx_wt.sum(axis=-1) + seg_wt.sum(axis=-1)]
    while x19 -> x0, local copies, waits for them, and re-layouts: 28.8 us -> none
    unnamed x28 -> x1, local copies, waits for them, and re-layouts: 9.7 us -> 2.16 us
  transfers between devices with their start and end apart: 15 -> 0, of which waited for: 3 -> 0; matrix products, arithmetic and copies ran while one was open for 29% -> 0% of each run, Pallas kernels for 0% -> 0%
where the time goes in v1:
time: 190 us
  Pallas kernels  183 us (96%)
  local copies, waits for them, and re-layouts  5.35 us (3%)
    pallas_call x1, Pallas kernels, device_fn(): pl.pallas_call(functools.partial(kernel, dims), out_shape=(jax.ShapeDtype...  183 us

profile of v1, /device:TPU:0, one launch (start us, length us, event | category | flops | bytes accessed | tf_op | source)
XLA Modules:
  0.0 189.6 jit_solution(3595128828840678192)
XLA Ops:
  1.3 182.9 %shard_map.121 = (bf16[128,3584]{1,0:T(8,128)(2,1)}, bf16[128,512]{1,0:T(8,128)(2,1)}, bf16[128,512]{1,0:T(8,128)(2,1)}) custom-call(s32[1]{0:T(128)S(6)} %copy.14.len_ref, bf16[128,3584]{1,0:T(8,128)(2,1)} %x_ref.1, bf16[4096,2,2,128]{3,2,1,0:T(2,128)(2,1)} %bitcast.2, bf16[4096,2,2,128]{3,2,1,0:T(2,128)(2,1)} %bitcast.3, bf16[3584,3584]{1,0:T(8,128)(2,1)} %wq_ref.1, ...), custom_call_target="tpu_custom_call" | custom-call | tf_op jit(solution)/shard_map/pallas_call | solution.py:301
  184.2 1.6 reshape.20
  185.8 1.6 reshape.21
  187.4 2.2 %copy.15 = bf16[128,3584]{1,0:T(8,128)(2,1)} copy(bf16[128,3584]{1,0:T(8,128)(2,1)} %get-tuple-element.12) | data formatting | bytes 1835008

commit v2 on v1

--- a/solution.py
+++ b/solution.py
@@ -12,7 +12,10 @@
 ROPE_BASE = 500000.0
 MESH = pl.DeviceIdType.MESH
 KEY_TILE = 1024
+SUB = 1024
+PV_SUBS = 1
 PREP = 128
+PREP_GROUPS = 4
 HIDE = -3e38
 
 
@@ -38,7 +41,7 @@
 
 
 def kernel(dims, len_ref, x_ref, k_ref, v_ref, wq_ref, wk_ref, wv_ref, wo_ref, cos_ref, sin_ref, y_ref, ko_ref, vo_ref,
-           xbuf, raw_k, raw_v, lens, kb, vt, kn, vtn, wbuf, wo1, cosb, sinb, qbuf, ob, pb, oall, ost, kvx,
+           xbuf, raw_k, raw_v, lens, kb, vt, kn, vtn, wbuf, wo1, cosb, sinb, qbuf, ob, pb, oall, ost, kvx, kvr, ybuf, s_scr, sn_scr, acc,
            loc_sem, wq_sem, pair_s, pair_r, q_s, q_r, p_s, p_r, o_s, o_r):
     heads, head_dim, group, tok, cache, cp_size = dims
     my_heads = heads // 2
@@ -73,9 +76,8 @@
     ld_wo0 = pltpu.make_async_copy(wo_ref.at[:, pl.ds(0, half_cols)], wbuf, loc_sem.at[7])
     ld_wo1 = pltpu.make_async_copy(wo_ref.at[:, pl.ds(half_cols, half_cols)], wo1, loc_sem.at[8])
     ld_x.start()
-    ld_wq(0).start()
-    ld_cos.start()
-    ld_sin.start()
+    ld_k.start()
+    ld_v.start()
     lens[0] = jnp.full(lens.shape[1:], len_ref[0], jnp.int32)
 
     barrier = pltpu.get_barrier_semaphore()
@@ -90,15 +92,50 @@
     cp_k = remote(k_ref.at[:, 1 - core], raw_k.at[1], pair_s.at[2], pair_r.at[2], mate)
     cp_v = remote(v_ref.at[:, 1 - core], raw_v.at[1], pair_s.at[3], pair_r.at[3], mate)
     cp_x.start()
-    for j in range(1, n_chunk):
+    cp_len.start()
+    for j in range(2):
         ld_wq(j).start()
-    cp_len.start()
     cp_k.start()
     cp_v.start()
+    for j in range(2, n_chunk):
+        ld_wq(j).start()
     ld_wk.start()
     ld_wv.start()
-    ld_k.start()
-    ld_v.start()
+    ld_cos.start()
+    ld_sin.start()
+
+    row = lax.broadcasted_iota(jnp.int32, (2 * PREP, 2 * PREP), 0)
+    col = lax.broadcasted_iota(jnp.int32, (2 * PREP, 2 * PREP), 1)
+    want = jnp.where(row < PREP, 2 * row, 2 * (row - PREP) + 1)
+    pick = jnp.where(col == want, 1.0, 0.0).astype(jnp.bfloat16)
+    want_back = jnp.where(col < PREP, 2 * col, 2 * (col - PREP) + 1)
+    weave = jnp.where(row == want_back, 1.0, 0.0).astype(jnp.bfloat16)
+    lane = lax.broadcasted_iota(jnp.int32, (PREP, head_dim), 1)
+    slot = lax.broadcasted_iota(jnp.int32, (PREP, head_dim), 0)
+
+    def prep(block):
+        flat_k = raw_k.at[block].reshape(2 * cache, head_dim)
+        flat_v = raw_v.at[block].reshape(2 * cache, head_dim)
+
+        def step(i, carry):
+            for g in range(PREP_GROUPS):
+                at = pl.multiple_of((i * PREP_GROUPS + g) * PREP, PREP)
+                to = pl.multiple_of(block * cache + at, PREP)
+                both = jnp.concatenate([flat_k[pl.ds(2 * at, 2 * PREP)], flat_v[pl.ds(2 * at, 2 * PREP)]], axis=1)
+                split = jnp.dot(pick, both, preferred_element_type=jnp.float32).astype(jnp.bfloat16)
+                hidden = jnp.where((slot + at >= lens[block, 0:1, :]) & (lane == 0), HIDE, 0.0).astype(jnp.bfloat16)
+                for h in range(2):
+                    part = split[h * PREP:(h + 1) * PREP]
+                    kb[h, pl.ds(to, PREP), :head_dim] = part[:, :head_dim]
+                    kb[h, pl.ds(to, PREP), head_dim:] = hidden
+                    vt[h, :, pl.ds(to, PREP)] = part[:, head_dim:].T
+            return carry
+
+        lax.fori_loop(0, cache // PREP // PREP_GROUPS, step, 0)
+
+    ld_k.wait()
+    ld_v.wait()
+    prep(0)
 
     def rope(vals):
         return vals * cosb[...] + pltpu.roll(vals, head_dim // 2, 1) * sinb[...]
@@ -112,67 +149,59 @@
     ld_sin.wait()
     cp_x.wait_recv()
 
-    def q_step(j, carry):
-        ld_wq(j).wait()
-        proj = jnp.dot(xbuf[...], wbuf[:, pl.ds(pl.multiple_of(j * pair, pair), pair)], preferred_element_type=jnp.float32)
-        qbuf[2 * j] = rope(proj[:, :head_dim]).astype(jnp.bfloat16)
-        qbuf[2 * j + 1] = rope(proj[:, head_dim:]).astype(jnp.bfloat16)
-        cp_q(j).start()
-        return carry
-
-    lax.fori_loop(0, n_chunk, q_step, 0)
+    chunks = [(2 * j, min(2, n_chunk - 2 * j)) for j in range((n_chunk + 1) // 2)]
+    for step in range(len(chunks) + 2):
+        if step < len(chunks):
+            first, count = chunks[step]
+            for j in range(first, first + count):
+                ld_wq(j).wait()
+            proj = jnp.dot(xbuf[...], wbuf[:, first * pair:(first + count) * pair], preferred_element_type=jnp.float32)
+        elif step == len(chunks):
+            ld_wk.wait()
+            ld_wv.wait()
+            proj = jnp.dot(xbuf[...], wo1[:, :2 * pair], preferred_element_type=jnp.float32)
+        if step >= 1 and step - 1 < len(chunks):
+            first, count = chunks[step - 1]
+            for j in range(first, first + count):
+                for h in range(2):
+                    part = s_scr[(step - 1) % 2, (j - first) * toks:(j - first + 1) * toks, h * head_dim:(h + 1) * head_dim]
+                    qbuf[2 * j + h] = rope(part).T.astype(jnp.bfloat16)
+                cp_q(j).start()
+        if step <= len(chunks):
+            for n in range(proj.shape[1] // pair):
+                s_scr[step % 2, n * toks:(n + 1) * toks] = proj[:, n * pair:(n + 1) * pair]
     ld_wo0.start()
-
-    ld_wk.wait()
-    ld_wv.wait()
-    k_proj = jnp.dot(xbuf[...], wo1[:, :pair], preferred_element_type=jnp.float32)
-    v_proj = jnp.dot(xbuf[...], wo1[:, pair:2 * pair], preferred_element_type=jnp.float32)
+    ld_wo1.start()
+    done = len(chunks) % 2
+    k_heads = [rope(s_scr[done, :toks, h * head_dim:(h + 1) * head_dim]).astype(jnp.bfloat16) for h in range(2)]
+    v_heads = [s_scr[done, toks:2 * toks, h * head_dim:(h + 1) * head_dim].astype(jnp.bfloat16) for h in range(2)]
     for h in range(2):
-        kn[h] = rope(k_proj[:, h * head_dim:(h + 1) * head_dim]).astype(jnp.bfloat16)
-        v_h = v_proj[:, h * head_dim:(h + 1) * head_dim].astype(jnp.bfloat16)
-        vtn[h] = v_proj[:, h * head_dim:(h + 1) * head_dim].T.astype(jnp.bfloat16)
-        kvx[0, :, h * head_dim:(h + 1) * head_dim] = kn[h]
-        kvx[1, :, h * head_dim:(h + 1) * head_dim] = v_h
-    ld_wo1.start()
-    cp_ko = remote(kvx.at[0, mate_rows], kvx.at[2, pl.ds(0, tok)], pair_s.at[4], pair_r.at[4], mate)
-    cp_vo = remote(kvx.at[1, mate_rows], kvx.at[2, pl.ds(tok, tok)], pair_s.at[5], pair_r.at[5], mate)
+        kn[h] = k_heads[h]
+        vtn[h] = v_heads[h].T
+    for part in range(2):
+        rows = slice(part * tok, (part + 1) * tok)
+        both = jnp.concatenate([jnp.concatenate([k_heads[h][rows], v_heads[h][rows]], axis=1) for h in range(2)], axis=0)
+        mixed = jnp.dot(weave, both, preferred_element_type=jnp.float32).astype(jnp.bfloat16)
+        for n in range(2):
+            kvx[n, rows] = mixed[:, n * head_dim:(n + 1) * head_dim].reshape(tok, 2, head_dim)
+    cp_ko = remote(kvx.at[0, mate_rows], kvr.at[0], pair_s.at[4], pair_r.at[4], mate)
+    cp_vo = remote(kvx.at[1, mate_rows], kvr.at[1], pair_s.at[5], pair_r.at[5], mate)
     cp_ko.start()
     cp_vo.start()
-
-    row = lax.broadcasted_iota(jnp.int32, (2 * PREP, 2 * PREP), 0)
-    col = lax.broadcasted_iota(jnp.int32, (2 * PREP, 2 * PREP), 1)
-    want = jnp.where(row < PREP, 2 * row, 2 * (row - PREP) + 1)
-    pick = jnp.where(col == want, 1.0, 0.0).astype(jnp.bfloat16)
-    lane = lax.broadcasted_iota(jnp.int32, (PREP, head_dim), 1)
-    slot = lax.broadcasted_iota(jnp.int32, (PREP, head_dim), 0)
-
-    def prep(block):
-        def step(i, carry):
-            at = pl.multiple_of(i * PREP, PREP)
-            to = pl.multiple_of(block * cache + i * PREP, PREP)
-            both = jnp.concatenate([raw_k[block, pl.ds(at, PREP)].reshape(2 * PREP, head_dim), raw_v[block, pl.ds(at, PREP)].reshape(2 * PREP, head_dim)], axis=1)
-            split = jnp.dot(pick, both, preferred_element_type=jnp.float32)
-            hidden = jnp.where((slot + at >= lens[block, 0:1, :]) & (lane == 0), HIDE, 0.0).astype(jnp.bfloat16)
-            for h in range(2):
-                part = split[h * PREP:(h + 1) * PREP]
-                kb[h, pl.ds(to, PREP), :head_dim] = part[:, :head_dim].astype(jnp.bfloat16)
-                kb[h, pl.ds(to, PREP), head_dim:] = hidden
-                vt[h, :, pl.ds(to, PREP)] = part[:, head_dim:].T.astype(jnp.bfloat16)
-            return carry
-
-        lax.fori_loop(0, cache // PREP, step, 0)
-
-    ld_k.wait()
-    ld_v.wait()
-    prep(0)
+    outs = [pltpu.make_async_copy(kvx.at[n, my_rows], out_ref.at[:, core], loc_sem.at[9 + n]) for n, out_ref in ((0, ko_ref), (1, vo_ref))]
+    for out in outs:
+        out.start()
+
     cp_len.wait_recv()
     cp_k.wait_recv()
     cp_v.wait_recv()
     prep(1)
 
     n_tiles = 2 * cache // KEY_TILE
+    n_sub = KEY_TILE // SUB
     first_a = 2
-    ones_col = jnp.where(lax.broadcasted_iota(jnp.int32, (toks, head_dim), 1) == 0, 1.0, 0.0).astype(jnp.bfloat16)
+    new_at = 3
+    ones_row = jnp.where(lax.broadcasted_iota(jnp.int32, (head_dim, toks), 0) == 0, 1.0, 0.0).astype(jnp.bfloat16)
 
     def positions(chip_id, axis):
         within = lax.broadcasted_iota(jnp.int32, (toks, toks), axis)
@@ -185,57 +214,106 @@
     def cp_p(h):
         return remote(ob.at[my_heads + h], pb.at[h], p_s.at[h], p_r.at[h], peer)
 
-    def attend(i, carry):
+    def place(i):
         is_b = jnp.logical_and(i >= first_a, i < first_a + my_heads)
         idx = jnp.where(i < first_a, i, jnp.where(is_b, my_heads + i - first_a, i - my_heads))
-        head = jnp.where(is_b, idx - my_heads, idx)
+        return is_b, idx, jnp.where(is_b, idx - my_heads, idx)
+
+    def peak(s):
+        return jnp.max(s.reshape(s.shape[0] // 8, 8, toks), axis=0)
+
+    def scores(kvh, q_aug, t, r):
+        s = jnp.dot(kb[kvh, t * KEY_TILE + r * SUB:t * KEY_TILE + (r + 1) * SUB], q_aug, preferred_element_type=jnp.float32)
+        s_scr[t % 2, r * SUB:(r + 1) * SUB] = s
+        return peak(s)
+
+    def with_ones(q):
+        return jnp.concatenate([q, ones_row], axis=0)
+
+    def attend(i, tops):
+        is_b, idx, head = place(i)
         kvh = lax.div(head, group)
         q_chip = jnp.where(is_b, 1 - chip, chip)
-
-        @pl.when(jnp.logical_and(is_b, lax.rem(head, 2) == 0))
+        after = jnp.minimum(i + 1, 2 * my_heads - 1)
+        next_b, next_idx, next_head = place(after)
+        next_kvh = lax.div(next_head, group)
+
+        @pl.when(jnp.logical_and(jnp.logical_and(next_b, after > i), lax.rem(next_head, 2) == 0))
         def _():
-            cp_q(lax.div(head, 2)).wait_recv()
-
-        q = qbuf[idx]
-        q_aug = jnp.concatenate([q, ones_col], axis=1)
+            cp_q(lax.div(next_head, 2)).wait_recv()
+
+        q_aug = with_ones(qbuf[idx])
+        next_q = with_ones(qbuf[next_idx])
+        tops = list(tops)
         top = None
-        for t in range(n_tiles + 1):
-            if t < n_tiles:
-                s = dot_t(kb[kvh, t * KEY_TILE:(t + 1) * KEY_TILE], q_aug)
-                vals = vt[kvh, :, t * KEY_TILE:(t + 1) * KEY_TILE]
-            else:
-                s = dot_t(kn[kvh], q)
+        total = None
+        for t in range(n_tiles):
+            here = tops[t]
+            if t == new_at:
+                here = jnp.maximum(here, seg_tops)
+            tile_top = jnp.max(here, axis=0, keepdims=True)
+            new_top = tile_top if top is None else jnp.maximum(top, tile_top)
+            keep = None if top is None else jnp.exp2((top - new_top) * score_c)
+            top = new_top
+            new_tops = None
+            w_sum = None
+            halves = []
+            for r in range(n_sub):
+                w = jnp.exp2((s_scr[t % 2, r * SUB:(r + 1) * SUB] - top) * score_c)
+                if t + 2 < n_tiles:
+                    sub_tops = scores(kvh, q_aug, t + 2, r)
+                else:
+                    sub_tops = scores(next_kvh, next_q, t + 2 - n_tiles, r)
+                new_tops = sub_tops if new_tops is None else jnp.maximum(new_tops, sub_tops)
+                part = jnp.sum(w.reshape(SUB // 8, 8, toks), axis=0)
+                w_sum = part if w_sum is None else w_sum + part
+                halves.append(w.astype(jnp.bfloat16))
+                if len(halves) == PV_SUBS:
+                    at = t * KEY_TILE + (r + 1 - PV_SUBS) * SUB
+                    wide = halves[0] if PV_SUBS == 1 else jnp.concatenate(halves, axis=0)
+                    halves = []
+                    out = jnp.dot(vt[kvh, :, at:at + PV_SUBS * SUB], wide, preferred_element_type=jnp.float32)
+                    if r + 1 > PV_SUBS:
+                        acc[...] += out
+                    elif keep is None:
+                        acc[...] = out
+                    else:
+                        acc[...] = acc[...] * keep + out
+            if t == new_at - 2:
+                s = jnp.dot(kn[kvh], qbuf[idx], preferred_element_type=jnp.float32)
                 s = jnp.where(positions(chip, 0) <= positions(q_chip, 1), s, -jnp.inf)
-                vals = vtn[kvh]
-            tile_top = jnp.max(s, axis=0, keepdims=True)
-            new_top = tile_top if top is None else jnp.maximum(top, tile_top)
-            w = jnp.exp2((s - new_top) * score_c)
-            w_sum = jnp.sum(w, axis=0, keepdims=True)
-            out = jnp.dot(vals, w.astype(jnp.bfloat16), preferred_element_type=jnp.float32)
-            if top is None:
-                total, acc = w_sum, out
-            else:
-                keep = jnp.exp2((top - new_top) * score_c)
-                total = total * keep + w_sum
-                acc = acc * keep + out
-            top = new_top
-        ob[idx, :head_dim] = acc
+                sn_scr[...] = s
+                seg_tops = peak(s)
+            if t == new_at:
+                w = jnp.exp2((sn_scr[...] - top) * score_c)
+                w_sum = w_sum + jnp.sum(w.reshape(toks // 8, 8, toks), axis=0)
+                acc[...] += jnp.dot(vtn[kvh], w.astype(jnp.bfloat16), preferred_element_type=jnp.float32)
+            total = w_sum if keep is None else total * keep + w_sum
+            tops.append(new_tops)
+        ob[idx, :head_dim] = acc[...]
         ob[idx, head_dim:head_dim + 8] = jnp.broadcast_to(top, (8, toks))
-        ob[idx, head_dim + 8:head_dim + 16] = jnp.broadcast_to(total, (8, toks))
+        ob[idx, head_dim + 8:head_dim + 16] = jnp.broadcast_to(jnp.sum(total, axis=0, keepdims=True), (8, toks))
 
         @pl.when(is_b)
         def _():
             cp_p(head).start()
 
-        return carry
-
-    lax.fori_loop(0, 2 * my_heads, attend, 0)
+        return tops[n_tiles], tops[n_tiles + 1]
+
+    first_q = with_ones(qbuf[0])
+    start_tops = []
+    for t in range(2):
+        tops = scores(0, first_q, t, 0)
+        for r in range(1, n_sub):
+            tops = jnp.maximum(tops, scores(0, first_q, t, r))
+        start_tops.append(tops)
+    lax.fori_loop(0, 2 * my_heads, attend, tuple(start_tops))
 
     cp_ko.wait()
     cp_vo.wait()
-    for out_ref, n in ((ko_ref, 0), (vo_ref, 1)):
-        out_ref[:, pl.ds(pl.multiple_of(core * pair, pair), pair)] = kvx[n, my_rows]
-        out_ref[:, pl.ds(pl.multiple_of((1 - core) * pair, pair), pair)] = kvx[2, n * tok:(n + 1) * tok]
+    more = [pltpu.make_async_copy(kvr.at[n], out_ref.at[:, 1 - core], loc_sem.at[11 + n]) for n, out_ref in ((0, ko_ref), (1, vo_ref))]
+    for out in more:
+        out.start()
 
     def cp_o(h):
         col = pl.multiple_of((core * my_heads + h) * head_dim, head_dim)
@@ -265,11 +343,17 @@
         return carry
 
     lax.fori_loop(0, my_heads, drain, 0)
+    y_copies = []
     for half, weights in ((0, wbuf), (1, wo1)):
         for n in range(half_cols // pair):
+            cols = slice(half * half_cols + n * pair, half * half_cols + (n + 1) * pair)
             part = jnp.dot(oall[...], weights[:, n * pair:(n + 1) * pair], preferred_element_type=jnp.float32)
-            y_ref[:, half * half_cols + n * pair:half * half_cols + (n + 1) * pair] = part.astype(jnp.bfloat16)
-
+            ybuf[:, cols] = part.astype(jnp.bfloat16)
+        cols = pl.ds(half * half_cols, half_cols)
+        y_copies.append(pltpu.make_async_copy(ybuf.at[:, cols], y_ref.at[:, cols], loc_sem.at[13 + half]))
+        y_copies[-1].start()
+    for out in y_copies + outs + more:
+        out.wait()
     for j in range(n_chunk):
         cp_q(j).wait_send()
     for copy in (cp_x, cp_len, cp_k, cp_v):
@@ -296,17 +380,16 @@
         k4 = k_cache.reshape(cache, 2, 2, head_dim)
         v4 = v_cache.reshape(cache, 2, 2, head_dim)
         any_spec = pl.BlockSpec(memory_space=pl.ANY)
-        vmem_spec = pl.BlockSpec(memory_space=pltpu.VMEM)
         dma = pltpu.SemaphoreType.DMA
         y_out, k_new, v_new = pl.pallas_call(
             functools.partial(kernel, dims),
             out_shape=(
                 jax.ShapeDtypeStruct((tok, width), bf16),
-                jax.ShapeDtypeStruct((tok, kv_heads * head_dim), bf16),
-                jax.ShapeDtypeStruct((tok, kv_heads * head_dim), bf16),
+                jax.ShapeDtypeStruct((tok, kv_heads // 2, 2, head_dim), bf16),
+                jax.ShapeDtypeStruct((tok, kv_heads // 2, 2, head_dim), bf16),
             ),
             in_specs=[pl.BlockSpec(memory_space=pltpu.SMEM)] + [any_spec] * 9,
-            out_specs=(vmem_spec,) * 3,
+            out_specs=(any_spec,) * 3,
             scratch_shapes=[
                 pltpu.VMEM((toks, width), bf16),
                 pltpu.VMEM((2, cache, 2, head_dim), bf16),
@@ -320,13 +403,18 @@
                 pltpu.VMEM((width, half_cols), bf16),
                 pltpu.VMEM((toks, head_dim), f32),
                 pltpu.VMEM((toks, head_dim), f32),
-                pltpu.VMEM((heads, toks, head_dim), bf16),
+                pltpu.VMEM((heads, head_dim, toks), bf16),
                 pltpu.VMEM((heads, head_dim + 16, toks), f32),
                 pltpu.VMEM((my_heads, head_dim + 16, toks), f32),
                 pltpu.VMEM((tok, heads * head_dim), bf16),
                 pltpu.VMEM((my_heads, toks, head_dim), bf16),
-                pltpu.VMEM((3, toks, 2 * head_dim), bf16),
-                dma((9,)), dma((my_heads // 2,)), dma((6,)), dma((6,)),
+                pltpu.VMEM((2, toks, 2, head_dim), bf16),
+                pltpu.VMEM((2, tok, 2, head_dim), bf16),
+                pltpu.VMEM((tok, width), bf16),
+                pltpu.VMEM((2, KEY_TILE, toks), f32),
+                pltpu.VMEM((toks, toks), f32),
+                pltpu.VMEM((head_dim, toks), f32),
+                dma((15,)), dma((my_heads // 2,)), dma((6,)), dma((6,)),
                 dma((my_heads // 2,)), dma((my_heads // 2,)),
                 dma((my_heads,)), dma((my_heads,)), dma((my_heads,)), dma((my_heads,)),
             ],

time: 190 us -> 101 us (0.53)
  Pallas kernels: 183 us -> 94.5 us
    pallas_call x1, Pallas kernels: 183 us -> 94.5 us  [device_fn(): pl.pallas_call(functools.partial(kernel, dims), out_shape=(jax.ShapeDtype...]
    unnamed x1 -> x3, local copies, waits for them, and re-layouts: 2.16 us -> 5.37 us
    reshape x2 -> x0, local copies, waits for them, and re-layouts: 3.19 us -> none  [device_fn(): return (y_out, k_new.reshape(shape), v_new.reshape(shape))]
where the time goes in v2:
time: 101 us
  Pallas kernels  94.5 us (94%)
  local copies, waits for them, and re-layouts  5.37 us (5%)
  between operations  1.29 us (1%)
    pallas_call x1, Pallas kernels, device_fn(): pl.pallas_call(functools.partial(kernel, dims), out_shape=(jax.ShapeDtype...  94.5 us
    unnamed x3, local copies, waits for them, and re-layouts  5.37 us

profile of v2, /device:TPU:0, one launch (start us, length us, event | category | flops | bytes accessed | tf_op | source)
XLA Modules:
  0.0 101.1 jit_solution(240821544051708394)
XLA Ops:
  1.3 94.5 %shard_map.121 = (bf16[128,3584]{1,0:T(8,128)(2,1)}, bf16[128,2,2,128]{3,2,1,0:T(2,128)(2,1)}, bf16[128,2,2,128]{3,2,1,0:T(2,128)(2,1)}) custom-call(s32[1]{0:T(128)S(6)} %copy.16.len_ref, bf16[128,3584]{1,0:T(8,128)(2,1)} %x_ref.1, bf16[4096,2,2,128]{3,2,1,0:T(2,128)(2,1)} %bitcast.4, bf16[4096,2,2,128]{3,2,1,0:T(2,128)(2,1)} %bitcast.5, ...), custom_call_target="tpu_custom_call" | custom-call | tf_op jit(solution)/shard_map/pallas_call | solution.py:384
  95.8 2.2 %copy.17 = bf16[128,3584]{1,0:T(8,128)(2,1)} copy(bf16[128,3584]{1,0:T(8,128)(2,1)} %get-tuple-element.12) | data formatting | bytes 1835008
  97.9 1.6 %copy.18 = bf16[128,4,128]{2,1,0:T(4,128)(2,1)} copy(bf16[128,4,128]{2,1,0:T(4,128)(2,1)} %bitcast.7) | data formatting | bytes 262144
  99.5 1.6 %copy.19 = bf16[128,4,128]{2,1,0:T(4,128)(2,1)} copy(bf16[128,4,128]{2,1,0:T(4,128)(2,1)} %bitcast.6) | data formatting | bytes 262144

commit v3 on v2

--- a/solution.py
+++ b/solution.py
@@ -66,15 +66,18 @@
     ld_v = pltpu.make_async_copy(v_ref.at[:, core], raw_v.at[0], loc_sem.at[4])
     n_chunk = my_heads // 2
 
-    def ld_wq(j):
+    def ld_wq(j, sem=None):
+        sem = j if sem is None else sem
         col = pl.multiple_of(core * half_cols + j * pair, pair)
-        return pltpu.make_async_copy(wq_ref.at[:, pl.ds(col, pair)], wbuf.at[:, pl.ds(pl.multiple_of(j * pair, pair), pair)], wq_sem.at[j])
+        return pltpu.make_async_copy(wq_ref.at[:, pl.ds(col, pair)], wbuf.at[:, pl.ds(pl.multiple_of(j * pair, pair), pair)], wq_sem.at[sem])
 
     kv_col = pl.multiple_of(core * pair, pair)
-    ld_wk = pltpu.make_async_copy(wk_ref.at[:, pl.ds(kv_col, pair)], wo1.at[:, pl.ds(0, pair)], loc_sem.at[5])
-    ld_wv = pltpu.make_async_copy(wv_ref.at[:, pl.ds(kv_col, pair)], wo1.at[:, pl.ds(pair, pair)], loc_sem.at[6])
-    ld_wo0 = pltpu.make_async_copy(wo_ref.at[:, pl.ds(0, half_cols)], wbuf, loc_sem.at[7])
-    ld_wo1 = pltpu.make_async_copy(wo_ref.at[:, pl.ds(half_cols, half_cols)], wo1, loc_sem.at[8])
+    ld_wk = pltpu.make_async_copy(wk_ref.at[:, pl.ds(kv_col, pair)], wbuf.at[:, pl.ds(half_cols, pair)], wq_sem.at[n_chunk])
+    ld_wv = pltpu.make_async_copy(wv_ref.at[:, pl.ds(kv_col, pair)], wbuf.at[:, pl.ds(half_cols + pair, pair)], wq_sem.at[n_chunk + 1])
+    wide = wbuf.shape[1]
+    rest = wo1.shape[1]
+    ld_wo0 = pltpu.make_async_copy(wo_ref.at[:, pl.ds(0, wide)], wbuf, loc_sem.at[7])
+    ld_wo1 = pltpu.make_async_copy(wo_ref.at[:, pl.ds(wide, rest)], wo1, loc_sem.at[8])
     ld_x.start()
     ld_k.start()
     ld_v.start()
@@ -149,32 +152,41 @@
     ld_sin.wait()
     cp_x.wait_recv()
 
-    chunks = [(2 * j, min(2, n_chunk - 2 * j)) for j in range((n_chunk + 1) // 2)]
-    for step in range(len(chunks) + 2):
-        if step < len(chunks):
-            first, count = chunks[step]
-            for j in range(first, first + count):
-                ld_wq(j).wait()
-            proj = jnp.dot(xbuf[...], wbuf[:, first * pair:(first + count) * pair], preferred_element_type=jnp.float32)
-        elif step == len(chunks):
-            ld_wk.wait()
-            ld_wv.wait()
-            proj = jnp.dot(xbuf[...], wo1[:, :2 * pair], preferred_element_type=jnp.float32)
-        if step >= 1 and step - 1 < len(chunks):
-            first, count = chunks[step - 1]
-            for j in range(first, first + count):
-                for h in range(2):
-                    part = s_scr[(step - 1) % 2, (j - first) * toks:(j - first + 1) * toks, h * head_dim:(h + 1) * head_dim]
-                    qbuf[2 * j + h] = rope(part).T.astype(jnp.bfloat16)
-                cp_q(j).start()
-        if step <= len(chunks):
-            for n in range(proj.shape[1] // pair):
-                s_scr[step % 2, n * toks:(n + 1) * toks] = proj[:, n * pair:(n + 1) * pair]
+    def project(first, count):
+        return jnp.dot(xbuf[...], wbuf[:, pl.ds(pl.multiple_of(first * pair, pair), count * pair)], preferred_element_type=jnp.float32)
+
+    def rotate(chunk, count):
+        for j in range(count):
+            for h in range(2):
+                part = s_scr[chunk % 2, j * toks:(j + 1) * toks, h * head_dim:(h + 1) * head_dim]
+                qbuf[4 * chunk + 2 * j + h] = rope(part).T.astype(jnp.bfloat16)
+
+    def proj_step(c, carry):
+        for j in (2 * c, 2 * c + 1):
+            ld_wq(jnp.minimum(j, n_chunk - 1), j).wait()
+        proj = project(2 * c, 2)
+        rotate(jnp.maximum(c - 1, 0), 2)
+        for n in range(2):
+            s_scr[c % 2, n * toks:(n + 1) * toks] = proj[:, n * pair:(n + 1) * pair]
+
+        @pl.when(c >= 1)
+        def _():
+            cp_q(2 * c - 2).start()
+            cp_q(2 * c - 1).start()
+
+        return carry
+
+    n_proj = (n_chunk + 1) // 2
+    lax.fori_loop(0, n_proj, proj_step, 0)
+    last = n_proj - 1
+    ld_wv.wait()
+    v_proj = project(n_chunk + 1, 1)
+    rotate(last, 1)
+    cp_q(n_chunk - 1).start()
     ld_wo0.start()
     ld_wo1.start()
-    done = len(chunks) % 2
-    k_heads = [rope(s_scr[done, :toks, h * head_dim:(h + 1) * head_dim]).astype(jnp.bfloat16) for h in range(2)]
-    v_heads = [s_scr[done, toks:2 * toks, h * head_dim:(h + 1) * head_dim].astype(jnp.bfloat16) for h in range(2)]
+    k_heads = [rope(s_scr[last % 2, toks:2 * toks, h * head_dim:(h + 1) * head_dim]).astype(jnp.bfloat16) for h in range(2)]
+    v_heads = [v_proj[:, h * head_dim:(h + 1) * head_dim].astype(jnp.bfloat16) for h in range(2)]
     for h in range(2):
         kn[h] = k_heads[h]
         vtn[h] = v_heads[h].T
@@ -215,9 +227,9 @@
         return remote(ob.at[my_heads + h], pb.at[h], p_s.at[h], p_r.at[h], peer)
 
     def place(i):
-        is_b = jnp.logical_and(i >= first_a, i < first_a + my_heads)
-        idx = jnp.where(i < first_a, i, jnp.where(is_b, my_heads + i - first_a, i - my_heads))
-        return is_b, idx, jnp.where(is_b, idx - my_heads, idx)
+        is_b = jnp.logical_and(i >= first_a, i < first_a + group)
+        j = jnp.where(i < first_a, i, jnp.where(is_b, i - first_a, i - group))
+        return is_b, jnp.where(is_b, my_heads + j, j), j
 
     def peak(s):
         return jnp.max(s.reshape(s.shape[0] // 8, 8, toks), axis=0)
@@ -230,18 +242,7 @@
     def with_ones(q):
         return jnp.concatenate([q, ones_row], axis=0)
 
-    def attend(i, tops):
-        is_b, idx, head = place(i)
-        kvh = lax.div(head, group)
-        q_chip = jnp.where(is_b, 1 - chip, chip)
-        after = jnp.minimum(i + 1, 2 * my_heads - 1)
-        next_b, next_idx, next_head = place(after)
-        next_kvh = lax.div(next_head, group)
-
-        @pl.when(jnp.logical_and(jnp.logical_and(next_b, after > i), lax.rem(next_head, 2) == 0))
-        def _():
-            cp_q(lax.div(next_head, 2)).wait_recv()
-
+    def one_head(kvh, idx, next_kvh, next_idx, tops, q_chip):
         q_aug = with_ones(qbuf[idx])
         next_q = with_ones(qbuf[next_idx])
         tops = list(tops)
@@ -294,11 +295,37 @@
         ob[idx, head_dim:head_dim + 8] = jnp.broadcast_to(top, (8, toks))
         ob[idx, head_dim + 8:head_dim + 16] = jnp.broadcast_to(jnp.sum(total, axis=0, keepdims=True), (8, toks))
 
+        return tops[n_tiles], tops[n_tiles + 1]
+
+    def attend(i, tops):
+        is_b, idx, j = place(i)
+        q_chip = jnp.where(is_b, 1 - chip, chip)
+        after = jnp.minimum(i + 1, 2 * group - 1)
+        next_b, next_idx, next_j = place(after)
+        fresh = jnp.logical_and(next_b, after > i)
+        odd = lax.rem(next_j, 2) == 1
+
+        @pl.when(jnp.logical_and(fresh, jnp.logical_and(jnp.logical_not(odd), next_j < group - 1)))
+        def _():
+            cp_q(lax.div(next_j, 2)).wait_recv()
+
+        @pl.when(jnp.logical_and(fresh, odd))
+        def _():
+            cp_q(lax.div(next_j + group, 2)).wait_recv()
+
+        @pl.when(jnp.logical_and(fresh, next_j == 0))
+        def _():
+            cp_q(group // 2).wait_recv()
+
+        tops = one_head(0, idx, 1, idx + group, tops, q_chip)
+        tops = one_head(1, idx + group, 0, next_idx, tops, q_chip)
+
         @pl.when(is_b)
         def _():
-            cp_p(head).start()
-
-        return tops[n_tiles], tops[n_tiles + 1]
+            cp_p(j).start()
+            cp_p(j + group).start()
+
+        return tops
 
     first_q = with_ones(qbuf[0])
     start_tops = []
@@ -307,7 +334,7 @@
         for r in range(1, n_sub):
             tops = jnp.maximum(tops, scores(0, first_q, t, r))
         start_tops.append(tops)
-    lax.fori_loop(0, 2 * my_heads, attend, tuple(start_tops))
+    lax.fori_loop(0, 2 * group, attend, tuple(start_tops))
 
     cp_ko.wait()
     cp_vo.wait()
@@ -337,6 +364,16 @@
     ld_wo0.wait()
     ld_wo1.wait()
 
+    own = pl.ds(pl.multiple_of(core * half_cols, half_cols), half_cols)
+    other = pl.ds(pl.multiple_of((1 - core) * half_cols, half_cols), half_cols)
+    spans = [(wbuf, n * pair, n * pair) for n in range(wide // pair)] + [(wo1, n * pair, wide + n * pair) for n in range(rest // pair)]
+
+    def y_part(weights, at, rows):
+        return jnp.dot(oall[:, rows], weights[rows, at:at + pair], preferred_element_type=jnp.float32)
+
+    for n, (weights, at, _) in enumerate(spans):
+        s_scr[n // 8, (n % 8) * tok:(n % 8 + 1) * tok] = y_part(weights, at, own)
+
     def drain(h, carry):
         cp_o(h).wait()
         cp_p(h).wait_send()
@@ -344,20 +381,39 @@
 
     lax.fori_loop(0, my_heads, drain, 0)
     y_copies = []
-    for half, weights in ((0, wbuf), (1, wo1)):
-        for n in range(half_cols // pair):
-            cols = slice(half * half_cols + n * pair, half * half_cols + (n + 1) * pair)
-            part = jnp.dot(oall[...], weights[:, n * pair:(n + 1) * pair], preferred_element_type=jnp.float32)
-            ybuf[:, cols] = part.astype(jnp.bfloat16)
-        cols = pl.ds(half * half_cols, half_cols)
-        y_copies.append(pltpu.make_async_copy(ybuf.at[:, cols], y_ref.at[:, cols], loc_sem.at[13 + half]))
-        y_copies[-1].start()
+    cuts = [len(spans) // 2, len(spans)]
+    for n, (weights, at, col) in enumerate(spans):
+        part = s_scr[n // 8, (n % 8) * tok:(n % 8 + 1) * tok] + y_part(weights, at, other)
+        ybuf[:, col:col + pair] = part.astype(jnp.bfloat16)
+        if n + 1 in cuts:
+            which = cuts.index(n + 1)
+            first = 0 if which == 0 else spans[cuts[which - 1]][2]
+            cols = pl.ds(first, col + pair - first)
+            y_copies.append(pltpu.make_async_copy(ybuf.at[:, cols], y_ref.at[:, cols], loc_sem.at[13 + which]))
+            y_copies[-1].start()
     for out in y_copies + outs + more:
         out.wait()
     for j in range(n_chunk):
         cp_q(j).wait_send()
     for copy in (cp_x, cp_len, cp_k, cp_v):
         copy.wait_send()
+
+
+def hand_on(y_in, k_in, v_in, y_ref, k_ref, v_ref, y_buf, k_buf, v_buf, in_sem, out_sem):
+    rows = y_in.shape[0] // 4
+    parts = [(src.at[...], buf.at[...], dst.at[...]) for src, buf, dst in ((k_in, k_buf, k_ref), (v_in, v_buf, v_ref))]
+    for n in range(4):
+        cut = pl.ds(n * rows, rows)
+        parts.append((y_in.at[cut], y_buf.at[cut], y_ref.at[cut]))
+    loads = [pltpu.make_async_copy(src, buf, in_sem.at[n]) for n, (src, buf, _) in enumerate(parts)]
+    stores = [pltpu.make_async_copy(buf, dst, out_sem.at[n]) for n, (_, buf, dst) in enumerate(parts)]
+    for load in loads:
+        load.start()
+    for load, store in zip(loads, stores):
+        load.wait()
+        store.start()
+    for store in stores:
+        store.wait()
 
 
 def solution(mesh):
@@ -399,8 +455,8 @@
                 pltpu.VMEM((2, head_dim, 2 * cache), bf16),
                 pltpu.VMEM((2, toks, head_dim), bf16),
                 pltpu.VMEM((2, head_dim, toks), bf16),
-                pltpu.VMEM((width, half_cols), bf16),
-                pltpu.VMEM((width, half_cols), bf16),
+                pltpu.VMEM((width, half_cols + 4 * head_dim), bf16),
+                pltpu.VMEM((width, heads * head_dim - half_cols - 4 * head_dim), bf16),
                 pltpu.VMEM((toks, head_dim), f32),
                 pltpu.VMEM((toks, head_dim), f32),
                 pltpu.VMEM((heads, head_dim, toks), bf16),
@@ -414,12 +470,19 @@
                 pltpu.VMEM((2, KEY_TILE, toks), f32),
                 pltpu.VMEM((toks, toks), f32),
                 pltpu.VMEM((head_dim, toks), f32),
-                dma((15,)), dma((my_heads // 2,)), dma((6,)), dma((6,)),
+                dma((15,)), dma((my_heads // 2 + 2,)), dma((6,)), dma((6,)),
                 dma((my_heads // 2,)), dma((my_heads // 2,)),
                 dma((my_heads,)), dma((my_heads,)), dma((my_heads,)), dma((my_heads,)),
             ],
             compiler_params=pltpu.CompilerParams(collective_id=0, has_side_effects=True, vmem_limit_bytes=67043328),
         )(valid_len, x_new, k4, v4, w_q, w_k, w_v, w_o, jnp.asarray(cos), jnp.asarray(sin))
+        y_out, k_new, v_new = pl.pallas_call(
+            hand_on,
+            out_shape=tuple(jax.ShapeDtypeStruct(part.shape, bf16) for part in (y_out, k_new, v_new)),
+            in_specs=[any_spec] * 3,
+            out_specs=(any_spec,) * 3,
+            scratch_shapes=[pltpu.VMEM(part.shape, bf16) for part in (y_out, k_new, v_new)] + [dma((6,)), dma((6,))],
+        )(y_out, k_new, v_new)
         shape = (tok, kv_heads, head_dim)
         return y_out, k_new.reshape(shape), v_new.reshape(shape)
 

time: 101 us -> 90.6 us (0.90)
  local copies, waits for them, and re-layouts: 5.37 us -> 0 us
  Pallas kernels: 94.5 us -> 89.2 us
    pallas_call x1, Pallas kernels: 94.5 us -> 87.1 us  [device_fn(): pl.pallas_call(functools.partial(kernel, dims), out_shape=(jax.ShapeDtype...]
    unnamed x3 -> x0, local copies, waits for them, and re-layouts: 5.37 us -> none
    pallas_call x0 -> x1, Pallas kernels: none -> 2.16 us  [device_fn(): pl.pallas_call(hand_on, out_shape=tuple((jax.ShapeDtypeStruct(part.shape,...]
where the time goes in v3:
time: 90.6 us; the launch traced here: 90.5 us
  Pallas kernels  89.2 us (98%)
  between operations  1.29 us (1%)
    pallas_call x1, Pallas kernels, device_fn(): pl.pallas_call(functools.partial(kernel, dims), out_shape=(jax.ShapeDtype...  87.1 us
    pallas_call x1, Pallas kernels, device_fn(): pl.pallas_call(hand_on, out_shape=tuple((jax.ShapeDtypeStruct(part.shape,...  2.16 us

profile of v3, /device:TPU:0, one launch (start us, length us, event | category | flops | bytes accessed | tf_op | source)
XLA Modules:
  0.0 90.5 jit_solution(3843904886837914916)
XLA Ops:
  1.3 87.1 %shard_map.121 = (bf16[128,3584]{1,0:T(8,128)(2,1)}, bf16[128,2,2,128]{3,2,1,0:T(2,128)(2,1)}, bf16[128,2,2,128]{3,2,1,0:T(2,128)(2,1)}) custom-call(s32[1]{0:T(128)S(6)} %copy.13.len_ref, bf16[128,3584]{1,0:T(8,128)(2,1)} %x_ref.1, bf16[4096,2,2,128]{3,2,1,0:T(2,128)(2,1)} %bitcast.4, bf16[4096,2,2,128]{3,2,1,0:T(2,128)(2,1)} %bitcast.5, ...), custom_call_target="tpu_custom_call" | custom-call | tf_op jit(solution)/shard_map/pallas_call | solution.py:440
  88.3 2.2 %shard_map.122 = (bf16[128,3584]{1,0:T(8,128)(2,1)}, bf16[128,2,2,128]{3,2,1,0:T(2,128)(2,1)}, bf16[128,2,2,128]{3,2,1,0:T(2,128)(2,1)}) custom-call(bf16[128,3584]{1,0:T(8,128)(2,1)} %get-tuple-element.9.y_in, bf16[128,2,2,128]{3,2,1,0:T(2,128)(2,1)} %get-tuple-element.10.k_in, bf16[128,2,2,128]{3,2,1,0:T(2,128)(2,1)} %get-tuple-element.11.v_in), custom_call_target="tpu_custom_call" | custom-call | tf_op jit(solution)/shard_map/pallas_call | solution.py:479

commit v4 on v3

--- a/solution.py
+++ b/solution.py
@@ -346,8 +346,7 @@
         col = pl.multiple_of((core * my_heads + h) * head_dim, head_dim)
         return remote(ost.at[h, mate_rows], oall.at[:, pl.ds(col, head_dim)], o_s.at[h], o_r.at[h], mate)
 
-    def combine(h, carry):
-        cp_p(h).wait_recv()
+    def combine_one(h):
         top_a, top_b = ob[h, head_dim:head_dim + 1], pb[h, head_dim:head_dim + 1]
         top = jnp.maximum(top_a, top_b)
         keep_a = jnp.exp2((top_a - top) * score_c)
@@ -355,12 +354,19 @@
         total = ob[h, head_dim + 8:head_dim + 9] * keep_a + pb[h, head_dim + 8:head_dim + 9] * keep_b
         out = (ob[h, :head_dim] * keep_a + pb[h, :head_dim] * keep_b) / total
         ost[h] = out.T.astype(jnp.bfloat16)
-        cp_o(h).start()
         col = pl.multiple_of((core * my_heads + h) * head_dim, head_dim)
         oall[:, pl.ds(col, head_dim)] = ost[h, my_rows]
+
+    def combine(j, carry):
+        for h in range(group):
+            cp_p(j * group + h).wait_recv()
+        for h in range(group):
+            combine_one(j * group + h)
+        for h in range(group):
+            cp_o(j * group + h).start()
         return carry
 
-    lax.fori_loop(0, my_heads, combine, 0)
+    lax.fori_loop(0, 2, combine, 0)
     ld_wo0.wait()
     ld_wo1.wait()
 

time: 90.6 us -> 89.4 us (0.987)
  Pallas kernels: 89.2 us -> 88 us
    pallas_call x1, Pallas kernels: 87.1 us -> 85.8 us  [device_fn(): pl.pallas_call(functools.partial(kernel, dims), out_shape=(jax.ShapeDtype...]
where the time goes in v4:
time: 89.4 us; the launch traced here: 89.2 us
  Pallas kernels  88 us (98%)
  between operations  1.29 us (1%)
    pallas_call x1, Pallas kernels, device_fn(): pl.pallas_call(functools.partial(kernel, dims), out_shape=(jax.ShapeDtype...  85.8 us
    pallas_call x1, Pallas kernels, device_fn(): pl.pallas_call(hand_on, out_shape=tuple((jax.ShapeDtypeStruct(part.shape,...  2.16 us

profile of v4, /device:TPU:0, one launch (start us, length us, event | category | flops | bytes accessed | tf_op | source)
XLA Modules:
  0.0 89.2 jit_solution(14367889255942971900)
XLA Ops:
  1.3 85.8 %shard_map.121 = (bf16[128,3584]{1,0:T(8,128)(2,1)}, bf16[128,2,2,128]{3,2,1,0:T(2,128)(2,1)}, bf16[128,2,2,128]{3,2,1,0:T(2,128)(2,1)}) custom-call(s32[1]{0:T(128)S(6)} %copy.13.len_ref, bf16[128,3584]{1,0:T(8,128)(2,1)} %x_ref.1, bf16[4096,2,2,128]{3,2,1,0:T(2,128)(2,1)} %bitcast.4, bf16[4096,2,2,128]{3,2,1,0:T(2,128)(2,1)} %bitcast.5, ...), custom_call_target="tpu_custom_call" | custom-call | tf_op jit(solution)/shard_map/pallas_call | solution.py:446
  87.1 2.2 %shard_map.122 = (bf16[128,3584]{1,0:T(8,128)(2,1)}, bf16[128,2,2,128]{3,2,1,0:T(2,128)(2,1)}, bf16[128,2,2,128]{3,2,1,0:T(2,128)(2,1)}) custom-call(bf16[128,3584]{1,0:T(8,128)(2,1)} %get-tuple-element.9.y_in, bf16[128,2,2,128]{3,2,1,0:T(2,128)(2,1)} %get-tuple-element.10.k_in, bf16[128,2,2,128]{3,2,1,0:T(2,128)(2,1)} %get-tuple-element.11.v_in), custom_call_target="tpu_custom_call" | custom-call | tf_op jit(solution)/shard_map/pallas_call | solution.py:485

commit v5 on v4

--- a/solution.py
+++ b/solution.py
@@ -79,6 +79,8 @@
     ld_wo0 = pltpu.make_async_copy(wo_ref.at[:, pl.ds(0, wide)], wbuf, loc_sem.at[7])
     ld_wo1 = pltpu.make_async_copy(wo_ref.at[:, pl.ds(wide, rest)], wo1, loc_sem.at[8])
     ld_x.start()
+    ld_cos.start()
+    ld_sin.start()
     ld_k.start()
     ld_v.start()
     lens[0] = jnp.full(lens.shape[1:], len_ref[0], jnp.int32)
@@ -104,8 +106,6 @@
         ld_wq(j).start()
     ld_wk.start()
     ld_wv.start()
-    ld_cos.start()
-    ld_sin.start()
 
     row = lax.broadcasted_iota(jnp.int32, (2 * PREP, 2 * PREP), 0)
     col = lax.broadcasted_iota(jnp.int32, (2 * PREP, 2 * PREP), 1)

time: 89.4 us -> 88.7 us (level)
  no operation moved by 1% of the time
where the time goes in v5:
time: 88.7 us; the launch traced here: 88.5 us
  Pallas kernels  87.2 us (98%)
  between operations  1.29 us (1%)
    pallas_call x1, Pallas kernels, device_fn(): pl.pallas_call(functools.partial(kernel, dims), out_shape=(jax.ShapeDtype...  85.1 us
    pallas_call x1, Pallas kernels, device_fn(): pl.pallas_call(hand_on, out_shape=tuple((jax.ShapeDtypeStruct(part.shape,...  2.16 us

profile of v5, /device:TPU:0, one launch (start us, length us, event | category | flops | bytes accessed | tf_op | source)
XLA Modules:
  0.0 88.5 jit_solution(1811260039492333025)
XLA Ops:
  1.3 85.1 %shard_map.121 = (bf16[128,3584]{1,0:T(8,128)(2,1)}, bf16[128,2,2,128]{3,2,1,0:T(2,128)(2,1)}, bf16[128,2,2,128]{3,2,1,0:T(2,128)(2,1)}) custom-call(s32[1]{0:T(128)S(6)} %copy.13.len_ref, bf16[128,3584]{1,0:T(8,128)(2,1)} %x_ref.1, bf16[4096,2,2,128]{3,2,1,0:T(2,128)(2,1)} %bitcast.4, bf16[4096,2,2,128]{3,2,1,0:T(2,128)(2,1)} %bitcast.5, ...), custom_call_target="tpu_custom_call" | custom-call | tf_op jit(solution)/shard_map/pallas_call | solution.py:446
  86.4 2.2 %shard_map.122 = (bf16[128,3584]{1,0:T(8,128)(2,1)}, bf16[128,2,2,128]{3,2,1,0:T(2,128)(2,1)}, bf16[128,2,2,128]{3,2,1,0:T(2,128)(2,1)}) custom-call(bf16[128,3584]{1,0:T(8,128)(2,1)} %get-tuple-element.9.y_in, bf16[128,2,2,128]{3,2,1,0:T(2,128)(2,1)} %get-tuple-element.10.k_in, bf16[128,2,2,128]{3,2,1,0:T(2,128)(2,1)} %get-tuple-element.11.v_in), custom_call_target="tpu_custom_call" | custom-call | tf_op jit(solution)/shard_map/pallas_call | solution.py:485
